TPU v7x, 32 devices: a whole 2x2x4 slice. The times are simulated.
32 devices in a mesh: dp: 2 (over x), ep: 16 (over z, y, core).
Axes of the slice: x: 2, y: 2, z: 4, core: 2. Of those that a mesh axis runs over, the one named last changes fastest.
Arguments:
- x_tokens: bfloat16 [4096, 2048], P(('dp', 'ep')), parts along dimension 0
- dy_tokens: bfloat16 [4096, 2048], P(('dp', 'ep')), parts along dimension 0
- expert_ids: int32 [4096, 10], P(('dp', 'ep')), parts along dimension 0
- gate_vals: float32 [4096, 10], P(('dp', 'ep')), parts along dimension 0
- slot_pos: int32 [4096, 10], P(('dp', 'ep')), parts along dimension 0
- w_gate: bfloat16 [32, 2048, 512], P('ep')
- w_up: bfloat16 [32, 2048, 512], P('ep')
- w_down: bfloat16 [32, 512, 2048], P('ep')
- shared_gate: bfloat16 [2048, 512], replicated
- shared_up: bfloat16 [2048, 512], replicated
- shared_down: bfloat16 [512, 2048], replicated
Outputs:
- output 1: bfloat16 [4096, 2048], P(('dp', 'ep')), parts along dimension 0
- output 2: float32 [64, 2048, 512], P(('dp', 'ep')), parts along dimension 0
- output 3: float32 [64, 2048, 512], P(('dp', 'ep')), parts along dimension 0
- output 4: float32 [64, 512, 2048], P(('dp', 'ep')), parts along dimension 0
- output 5: float32 [32, 2048, 512], P(('dp', 'ep')), parts along dimension 0
- output 6: float32 [32, 2048, 512], P(('dp', 'ep')), parts along dimension 0
- output 7: float32 [32, 512, 2048], P(('dp', 'ep')), parts along dimension 0
There are 2 independent parts. A program takes and returns all parts, laid end to end along the dimension named above; an argument that names none is the same for every part.
All inputs are finite; a program needn't handle non-finite values.
Results may differ from a plain program's by a relative error of at most 0.0104941.
Values are sent between devices in bfloat16 or wider.
A program may use at most 1 GiB of HBM per device.

v0:
```python
import jax
import jax.numpy as jnp
from jax import lax
from jax.sharding import PartitionSpec as P


def swiglu_parts(act_gate, act_up, grad_hidden):
    gate_f32 = act_gate.astype(jnp.float32)
    up_f32 = act_up.astype(jnp.float32)
    sigma = jax.nn.sigmoid(gate_f32)
    silu_gate = gate_f32 * sigma
    hidden = (silu_gate * up_f32).astype(jnp.bfloat16)
    grad_gate = (grad_hidden * up_f32 * sigma * (1.0 + gate_f32 * (1.0 - sigma))).astype(jnp.bfloat16)
    grad_up = (grad_hidden * silu_gate).astype(jnp.bfloat16)
    return hidden, grad_gate, grad_up


def slot_tables(expert_ids, slot_pos, gate_vals, num_experts, capacity):
    tok_count, top_k = expert_ids.shape
    slot_total = num_experts * capacity
    copy_slot = jnp.where(slot_pos >= 0, expert_ids * capacity + slot_pos, slot_total).reshape(-1)
    copy_token = jnp.broadcast_to(jnp.arange(tok_count, dtype=jnp.int32)[:, None], (tok_count, top_k)).reshape(-1)
    slot_token = jnp.full((slot_total + 1,), tok_count, jnp.int32).at[copy_slot].set(copy_token)[:slot_total]
    slot_gate = jnp.zeros((slot_total + 1,), jnp.float32).at[copy_slot].set(gate_vals.reshape(-1))[:slot_total]
    return copy_slot, slot_token, slot_gate


def take_rows(rows, row_index):
    return jnp.take(rows, row_index, axis=0, mode='fill', fill_value=0)


def shared_backward(x_tokens, dy_tokens, shared_gate, shared_up, shared_down):
    act_gate = jnp.dot(x_tokens, shared_gate, preferred_element_type=jnp.float32).astype(jnp.bfloat16)
    act_up = jnp.dot(x_tokens, shared_up, preferred_element_type=jnp.float32).astype(jnp.bfloat16)
    grad_hidden = jnp.einsum('td,fd->tf', dy_tokens, shared_down, preferred_element_type=jnp.float32)
    hidden, grad_gate, grad_up = swiglu_parts(act_gate, act_up, grad_hidden)
    grad_gate_w = jnp.einsum('td,tf->df', x_tokens, grad_gate, preferred_element_type=jnp.float32)
    grad_up_w = jnp.einsum('td,tf->df', x_tokens, grad_up, preferred_element_type=jnp.float32)
    grad_down_w = jnp.einsum('tf,td->fd', hidden, dy_tokens, preferred_element_type=jnp.float32)
    grad_input = jnp.einsum('tf,df->td', grad_gate, shared_gate, preferred_element_type=jnp.float32) + jnp.einsum('tf,df->td', grad_up, shared_up, preferred_element_type=jnp.float32)
    return grad_input, grad_gate_w, grad_up_w, grad_down_w


def solution(mesh):
    group = mesh.shape['ep']
    token_spec = P(('dp', 'ep'), None)
    expert_spec = P('ep', None, None)
    whole_spec = P(None, None)
    grad_spec = P(('dp', 'ep'), None, None)

    def local_backward(x_tokens, dy_tokens, expert_ids, gate_vals, slot_pos, w_gate, w_up, w_down, shared_gate, shared_up, shared_down):
        tok_count, top_k = expert_ids.shape
        local_experts, model_dim, expert_ff = w_gate.shape
        num_experts = local_experts * group
        capacity = (3 * tok_count * top_k + 2 * num_experts - 1) // (2 * num_experts)
        copy_slot, slot_token, slot_gate = slot_tables(expert_ids, slot_pos, gate_vals, num_experts, capacity)
        send_x = take_rows(x_tokens, slot_token).reshape(num_experts, capacity, model_dim)
        dy_rows = take_rows(dy_tokens, slot_token)
        send_dz = (dy_rows.astype(jnp.float32) * slot_gate[:, None]).astype(jnp.bfloat16).reshape(num_experts, capacity, model_dim)
        x_exp = lax.all_to_all(send_x, 'ep', 0, 1, tiled=True)
        dz_exp = lax.all_to_all(send_dz, 'ep', 0, 1, tiled=True)
        act_gate = jnp.einsum('erd,edf->erf', x_exp, w_gate, preferred_element_type=jnp.float32).astype(jnp.bfloat16)
        act_up = jnp.einsum('erd,edf->erf', x_exp, w_up, preferred_element_type=jnp.float32).astype(jnp.bfloat16)
        grad_hidden = jnp.einsum('erd,efd->erf', dz_exp, w_down, preferred_element_type=jnp.float32)
        hidden, grad_gate, grad_up = swiglu_parts(act_gate, act_up, grad_hidden)
        grad_w_gate = jnp.einsum('erd,erf->edf', x_exp, grad_gate, preferred_element_type=jnp.float32)
        grad_w_up = jnp.einsum('erd,erf->edf', x_exp, grad_up, preferred_element_type=jnp.float32)
        grad_w_down = jnp.einsum('erf,erd->efd', hidden, dz_exp, preferred_element_type=jnp.float32)
        grad_exp = (jnp.einsum('erf,edf->erd', grad_gate, w_gate, preferred_element_type=jnp.float32) + jnp.einsum('erf,edf->erd', grad_up, w_up, preferred_element_type=jnp.float32)).astype(jnp.bfloat16)
        returned = lax.all_to_all(grad_exp, 'ep', 1, 0, tiled=True).reshape(num_experts * capacity, model_dim)
        copies = take_rows(returned, copy_slot).reshape(tok_count, top_k, model_dim)
        routed_sum = jnp.sum(copies.astype(jnp.float32), axis=1)
        shared_dx, grad_shared_gate, grad_shared_up, grad_shared_down = shared_backward(x_tokens, dy_tokens, shared_gate, shared_up, shared_down)
        grad_x = (routed_sum + shared_dx).astype(jnp.bfloat16)
        return grad_x, grad_w_gate, grad_w_up, grad_w_down, grad_shared_gate[None], grad_shared_up[None], grad_shared_down[None]

    return jax.shard_map(local_backward, mesh=mesh, in_specs=(token_spec, token_spec, token_spec, token_spec, token_spec, expert_spec, expert_spec, expert_spec, whole_spec, whole_spec, whole_spec), out_specs=(token_spec, grad_spec, grad_spec, grad_spec, grad_spec, grad_spec, grad_spec), check_vma=False)
```

profile of v0, /device:TPU:15, one launch (start us, length us, event | category | flops | bytes accessed | tf_op | source)
XLA Modules:
  0.0 720.0 jit_solution(10129416709413290206)
XLA Ops:
  7.9 17.4 %gather_fusion.2 = bf16[1920,2048]{1,0:T(8,128)(2,1)} fusion(bf16[128,2048]{1,0:T(8,128)(2,1)} %param.13, s32[2048]{0:T(1024)S(1)} %pad_clamp_fusion.1), kind=kCustom, calls=%fused_computation.1.clone | custom fusion | bytes 15736320 | tf_op jit(solution)/shard_map/jit(_take)/gather | solution.py:29
  25.2 7.1 broadcast_select_fusion
  32.3 9.1 %reshape.105 = bf16[32,60,2048]{2,1,0:T(8,128)(2,1)} reshape(bf16[1920,2048]{1,0:T(8,128)(2,1)} %broadcast_select_fusion) | data formatting | bytes 15728640 | tf_op jit(solution)/shard_map/reshape | solution.py:57
  41.4 6.7 all-to-all-start.1
  48.1 8.6 %gather_fusion.1 = bf16[1920,2048]{1,0:T(8,128)(2,1)} fusion(bf16[128,2048]{1,0:T(8,128)(2,1)S(1)} %copy-done.2, s32[2048]{0:T(1024)S(1)} %pad_clamp_fusion.1), kind=kCustom, calls=%fused_computation.clone | custom fusion | bytes 15736320 | tf_op jit(solution)/shard_map/jit(_take)/gather | solution.py:29
  62.2 7.6 %multiply_convert_fusion = bf16[1920,2048]{1,0:T(8,128)(2,1)} fusion(bf16[1920,2048]{1,0:T(8,128)(2,1)} %gather_fusion.1, f32[1920]{0:T(1024)S(1)} %bitcast.54, pred[1920]{0:T(1024)(128)(4,1)S(1)} %compare_and_fusion), kind=kLoop, calls=%fused_computation.7 | loop fusion | flops 15728640 | bytes 15738240 | tf_op jit(solution)/shard_map/convert_element_type | solution.py:59
  69.8 9.1 %reshape.104 = bf16[32,60,2048]{2,1,0:T(8,128)(2,1)} reshape(bf16[1920,2048]{1,0:T(8,128)(2,1)} %multiply_convert_fusion) | data formatting | bytes 15728640 | tf_op jit(solution)/shard_map/reshape | solution.py:59
  79.0 151.7 %all-to-all-done.1 = bf16[32,60,2048]{2,1,0:T(8,128)(2,1)} async-done(((bf16[32,60,2048]{2,1,0:T(8,128)(2,1)}), bf16[32,60,2048]{2,1,0:T(8,128)(2,1)}, u32[]{:S(2)}, u32[]{:S(2)}) %all-to-all-start.1) | async-done | bytes 7864352 | tf_op jit(solution)/shard_map/all_to_all | solution.py:60
  235.8 14.7 %copy.59 = bf16[16,2,60,2048]{3,1,2,0:T(2,128)(2,1)S(1)} copy(bf16[16,2,60,2048]{3,2,1,0:T(8,128)(2,1)} %bitcast.4) | data formatting | bytes 15728640 | tf_op jit(solution)/shard_map/all_to_all | solution.py:60
  263.1 155.2 %all-to-all-done = bf16[32,60,2048]{2,1,0:T(8,128)(2,1)} async-done(((bf16[32,60,2048]{2,1,0:T(8,128)(2,1)}), bf16[32,60,2048]{2,1,0:T(8,128)(2,1)}, u32[]{:S(2)}, u32[]{:S(2)}) %all-to-all-start) | async-done | bytes 7864352 | tf_op jit(solution)/shard_map/all_to_all | solution.py:61
  418.3 14.6 %copy.57 = bf16[16,2,60,2048]{3,1,2,0:T(2,128)(2,1)S(1)} copy(bf16[16,2,60,2048]{3,2,1,0:T(8,128)(2,1)} %bitcast) | data formatting | bytes 15728640 | tf_op jit(solution)/shard_map/all_to_all | solution.py:61
  432.9 14.8 %fusion.14 = (bf16[2,960,512]{2,1,0:T(8,128)(2,1)}, f32[2,960,512]{2,1,0:T(8,128)}) fusion(bf16[2,960,512]{2,1,0:T(8,128)(2,1)} %fusion.23, bf16[2,960,512]{2,1,0:T(8,128)(2,1)} %fusion.26, bf16[2,512,2048]{2,1,0:T(8,128)(2,1)} %param.20, bf16[2,960,2048]{2,0,1:T(2,128)(2,1)S(1)} %bitcast.50), kind=kOutput, calls=%fused_computation.28 | convolution fusion | flops 4038328320 | bytes 21889024 | tf_op jit(solution)/shard_map/erd,efd->erf/dot_general | solution.py:64
  447.7 12.7 %fusion.41 = f32[2,960,2048]{2,1,0:T(8,128)} fusion(bf16[2,960,512]{2,1,0:T(8,128)(2,1)} %get-tuple-element.35, bf16[2,2048,512]{2,1,0:T(8,128)(2,1)} %param.18), kind=kOutput, calls=%fused_computation.69 | convolution fusion | flops 4026531840 | bytes 21889024 | tf_op jit(solution)/shard_map/erf,edf->erd/dot_general | solution.py:69
  460.4 12.1 %add_convert_fusion = bf16[2,960,2048]{2,1,0:T(8,128)(2,1)} fusion(f32[2,960,2048]{2,1,0:T(8,128)} %fusion.41, bf16[2,2048,512]{2,1,0:T(8,128)(2,1)} %param.19, f32[2,960,512]{2,1,0:T(8,128)} %get-tuple-element.36, bf16[2,960,512]{2,1,0:T(8,128)(2,1)S(1)} %copy-done.17), kind=kOutput, calls=%fused_computation.6 | convolution fusion | flops 4041277440 | bytes 33685504 | tf_op jit(solution)/shard_map/erf,edf->erd/dot_general | solution.py:69
  472.5 15.5 %copy.49 = bf16[2,960,2048]{2,0,1:T(2,128)(2,1)} copy(bf16[2,960,2048]{2,1,0:T(8,128)(2,1)} %add_convert_fusion) | data formatting | bytes 15728640 | tf_op jit(solution)/shard_map/convert_element_type | solution.py:69
  518.8 23.1 %fusion.6 = f32[2,2048,512]{2,1,0:T(8,128)} fusion(bf16[2,960,512]{2,1,0:T(8,128)(2,1)S(1)} %copy-done.16, bf16[2,960,2048]{2,0,1:T(2,128)(2,1)} %bitcast.48), kind=kOutput, calls=%fused_computation.18 | convolution fusion | flops 4026531840 | bytes 18219008 | tf_op jit(solution)/shard_map/erd,erf->edf/dot_general | solution.py:66
  541.9 11.4 %fusion = f32[2,512,2048]{2,1,0:T(8,128)} fusion(bf16[2,960,2048]{2,0,1:T(2,128)(2,1)S(1)} %bitcast.53, bf16[2,960,512]{2,1,0:T(8,128)(2,1)} %fusion.23, bf16[2,960,512]{2,1,0:T(8,128)(2,1)} %fusion.26), kind=kOutput, calls=%fused_computation.9 | convolution fusion | flops 4034396160 | bytes 20185088 | tf_op jit(solution)/shard_map/erf,erd->efd/dot_general | solution.py:68
  553.3 15.7 %fusion.4 = f32[2,2048,512]{2,1,0:T(8,128)} fusion(bf16[2,960,2048]{2,0,1:T(2,128)(2,1)} %bitcast.49, f32[2,960,512]{2,1,0:T(8,128)} %get-tuple-element.36, bf16[2,960,512]{2,1,0:T(8,128)(2,1)S(1)} %copy-done.18), kind=kOutput, calls=%fused_computation.16 | convolution fusion | flops 4033413120 | bytes 22151168 | tf_op jit(solution)/shard_map/erd,erf->edf/dot_general | solution.py:67
  569.0 95.2 %all-to-all-done.2 = bf16[2,960,2048]{2,0,1:T(2,128)(2,1)} async-done(((bf16[2,960,2048]{2,0,1:T(2,128)(2,1)}), bf16[2,960,2048]{2,0,1:T(2,128)(2,1)}, u32[]{:S(2)}, u32[]{:S(2)}) %all-to-all-start.2) | async-done | bytes 7864352 | tf_op jit(solution)/shard_map/all_to_all | solution.py:70
  664.2 10.5 %copy.50 = bf16[16,2,60,2048]{3,2,1,0:T(8,128)(2,1)} copy(bf16[16,2,60,2048]{3,1,2,0:T(2,128)(2,1)} %bitcast.10) | data formatting | bytes 15728640 | tf_op jit(solution)/shard_map/all_to_all | solution.py:70
  674.8 9.2 %reshape.106 = bf16[1920,2048]{1,0:T(8,128)(2,1)} reshape(bf16[16,2,60,2048]{3,2,1,0:T(8,128)(2,1)} %copy.50) | data formatting | bytes 15728640 | tf_op jit(solution)/shard_map/reshape | solution.py:70
  684.0 15.1 %gather_fusion = bf16[1280,2048]{1,0:T(8,128)(2,1)} fusion(bf16[1920,2048]{1,0:T(8,128)(2,1)} %reshape.106, s32[2048]{0:T(1024)S(1)} %pad_clamp_fusion), kind=kCustom, calls=%fused_computation.2 | custom fusion | bytes 10490880 | tf_op jit(solution)/shard_map/jit(_take)/gather | solution.py:29
  699.0 9.6 %gather.10 = bf16[128,10,2048]{2,1,0:T(8,128)(2,1)} reshape(bf16[1280,2048]{1,0:T(8,128)(2,1)} %gather_fusion) | data formatting | bytes 10485760 | tf_op jit(solution)/shard_map/jit(_take)/gather | solution.py:29
  708.6 9.3 %convert_reduce_fusion = f32[128,2048]{1,0:T(8,128)S(1)} fusion(bf16[128,10,2048]{2,1,0:T(8,128)(2,1)} %gather.10, pred[128,10]{1,0:T(8,128)(4,1)S(1)} %copy.39), kind=kLoop, calls=%fused_computation.5 | loop fusion | flops 7602176 | bytes 6292736 | tf_op jit(solution)/shard_map/reduce_sum | solution.py:72
  (72 shorter events, 62.7 us)
Async XLA Ops:
  0.6 492.4 %copy-start = (bf16[2048,512]{1,0:T(8,128)(2,1)S(1)}, bf16[2048,512]{1,0:T(8,128)(2,1)}, u32[]{:S(2)}) copy-start(bf16[2048,512]{1,0:T(8,128)(2,1)} %param.21) | copy-start | bytes 6291460
  41.4 6.7 copy-start.2
  41.4 189.3 %all-to-all-start.1 = ((bf16[32,60,2048]{2,1,0:T(8,128)(2,1)}), bf16[32,60,2048]{2,1,0:T(8,128)(2,1)}, u32[]{:S(2)}, u32[]{:S(2)}) async-start(bf16[32,60,2048]{2,1,0:T(8,128)(2,1)} %reshape.105), calls=%async_computation.1 | async-start | bytes 16777216 | tf_op jit(solution)/shard_map/all_to_all | solution.py:60
  48.1 8.7 %copy-start.12 = (f32[128,10]{0,1:T(8,128)S(1)}, f32[128,10]{0,1:T(8,128)}, u32[]{:S(2)}) copy-start(f32[128,10]{0,1:T(8,128)} %param.16) | copy-start | bytes 15364
  230.7 187.6 %all-to-all-start = ((bf16[32,60,2048]{2,1,0:T(8,128)(2,1)}), bf16[32,60,2048]{2,1,0:T(8,128)(2,1)}, u32[]{:S(2)}, u32[]{:S(2)}) async-start(bf16[32,60,2048]{2,1,0:T(8,128)(2,1)} %reshape.104), calls=%async_computation | async-start | bytes 16777216 | tf_op jit(solution)/shard_map/all_to_all | solution.py:61
  235.8 14.8 %copy-start.13 = (bf16[2,2048,512]{2,1,0:T(8,128)(2,1)S(1)}, bf16[2,2048,512]{2,1,0:T(8,128)(2,1)}, u32[]{:S(2)}) copy-start(bf16[2,2048,512]{2,1,0:T(8,128)(2,1)} %param.18) | copy-start | bytes 12582916
  250.6 6.4 copy-start.4
  250.6 6.4 copy-start.14
  432.8 14.8 %copy-start.5 = (bf16[16,2,60,2048]{3,1,2,0:T(2,128)(2,1)}, bf16[16,2,60,2048]{3,1,2,0:T(2,128)(2,1)S(1)}, u32[]{:S(2)}) copy-start(bf16[16,2,60,2048]{3,1,2,0:T(2,128)(2,1)S(1)} %copy.57) | copy-start | bytes 23592964
  447.7 12.7 %copy-start.17 = (bf16[2,960,512]{2,1,0:T(8,128)(2,1)S(1)}, bf16[2,960,512]{2,1,0:T(8,128)(2,1)}, u32[]{:S(2)}) copy-start(bf16[2,960,512]{2,1,0:T(8,128)(2,1)} %fusion.26) | copy-start | bytes 5898244
  488.0 5.0 copy-start.1
  488.0 176.3 %all-to-all-start.2 = ((bf16[2,960,2048]{2,0,1:T(2,128)(2,1)}), bf16[2,960,2048]{2,0,1:T(2,128)(2,1)}, u32[]{:S(2)}, u32[]{:S(2)}) async-start(bf16[2,960,2048]{2,0,1:T(2,128)(2,1)} %copy.49), calls=%async_computation.2 | async-start | bytes 15728640 | tf_op jit(solution)/shard_map/all_to_all | solution.py:70
  493.0 3.4 copy-start.15
  495.7 0.7 copy-start.7
  497.3 0.7 copy-start.9
  508.8 5.4 copy-start.11
  508.8 5.4 copy-start.8
  514.2 2.8 copy-start.10
  514.2 4.6 copy-start.16
  517.0 24.9 %slice-start = ((s8[7864320]{0:T(1024)(128)(4,1)}), s8[4194304]{0:T(1024)(128)(4,1)S(1)}, s32[]{:S(2)}) async-start(s8[7864320]{0:T(1024)(128)(4,1)} %bitcast.51), calls=%async_computation.3 | async-start | bytes 8388608
  518.8 23.1 %slice-start.1 = ((s8[7864320]{0:T(1024)(128)(4,1)}), s8[3670016]{0:T(1024)(128)(4,1)S(1)}, s32[]{:S(2)}) async-start(s8[7864320]{0:T(1024)(128)(4,1)} %bitcast.51), calls=%async_computation.4 | async-start | bytes 7340032
  541.9 11.4 %copy-start.18 = (bf16[2,960,512]{2,1,0:T(8,128)(2,1)S(1)}, bf16[2,960,512]{2,1,0:T(8,128)(2,1)}, u32[]{:S(2)}) copy-start(bf16[2,960,512]{2,1,0:T(8,128)(2,1)} %fusion.26) | copy-start | bytes 5898244
  708.6 9.3 %copy-start.3 = (bf16[2048,512]{1,0:T(8,128)(2,1)S(1)}, bf16[2048,512]{1,0:T(8,128)(2,1)}, u32[]{:S(2)}) copy-start(bf16[2048,512]{1,0:T(8,128)(2,1)} %param.22) | copy-start | bytes 6291460
  708.6 9.3 %copy-start.6 = (f32[128,2048]{1,0:T(8,128)S(1)}, f32[128,2048]{1,0:T(8,128)}, u32[]{:S(2)}) copy-start(f32[128,2048]{1,0:T(8,128)} %fusion.42) | copy-start | bytes 3145732
where the time goes:
time: 727 us; the launch traced here: 720 us
  waiting for transfers between devices  402 us (55%)
  local copies, waits for them, and re-layouts  157 us (22%)
  matrix products  117 us (16%)
  other arithmetic  25.5 us (4%)
  starting transfers between devices  16.7 us (2%)
    all_to_all x1, waiting for transfers between devices, local_backward(): dz_exp = lax.all_to_all(send_dz, 'ep', 0, 1, tiled=True)  155 us
    all_to_all x1, waiting for transfers between devices, local_backward(): x_exp = lax.all_to_all(send_x, 'ep', 0, 1, tiled=True)  152 us
    all_to_all x1, waiting for transfers between devices, local_backward(): lax.all_to_all(grad_exp, 'ep', 1, 0, tiled=True)  95.2 us
    gather x4, local copies, waits for them, and re-layouts, take_rows(): return jnp.take(rows, row_index, axis=0, mode='fill', fill_value=0)  50.6 us
    dot_general x1, matrix products, local_backward(): jnp.einsum('erd,erf->edf', x_exp, grad_gate, preferred_element_type=jnp.f...  23.1 us
    dot_general x1, matrix products, local_backward(): jnp.einsum('erd,erf->edf', x_exp, grad_up, preferred_element_type=jnp.flo...  15.7 us
    convert_element_type x1, local copies, waits for them, and re-layouts, local_backward(): (jnp.einsum('erf,edf->erd', grad_gate, w_gate, preferred_element_type=jnp...  15.5 us
    dot_general x1, matrix products, local_backward(): jnp.einsum('erd,efd->erf', dz_exp, w_down, preferred_element_type=jnp.flo...  14.8 us
  transfers between devices with their start and end apart: 3, of which 3 were waited for; matrix products, arithmetic and copies ran while one was open for 18% of the time, Pallas kernels for 0%

commit v1 on v0

v1 whole, which is shorter than its diff:
```python
import jax
import jax.numpy as jnp
from jax import lax
from jax.sharding import PartitionSpec as P

F32 = jnp.float32
BF16 = jnp.bfloat16


def swiglu_parts(act_gate, act_up, grad_hidden):
    gate_f32 = act_gate.astype(F32)
    up_f32 = act_up.astype(F32)
    sigma = jax.nn.sigmoid(gate_f32)
    silu_gate = gate_f32 * sigma
    hidden = (silu_gate * up_f32).astype(BF16)
    grad_gate = (grad_hidden * up_f32 * sigma * (1.0 + gate_f32 * (1.0 - sigma))).astype(BF16)
    grad_up = (grad_hidden * silu_gate).astype(BF16)
    return hidden, grad_gate, grad_up


def dot32(spec, a, b):
    return jnp.einsum(spec, a, b, preferred_element_type=F32)


def shared_backward(x_tokens, dy_tokens, shared_gate, shared_up, shared_down):
    act_gate = dot32('td,df->tf', x_tokens, shared_gate).astype(BF16)
    act_up = dot32('td,df->tf', x_tokens, shared_up).astype(BF16)
    grad_hidden = dot32('td,fd->tf', dy_tokens, shared_down)
    hidden, grad_gate, grad_up = swiglu_parts(act_gate, act_up, grad_hidden)
    grad_gate_w = dot32('td,tf->df', x_tokens, grad_gate)
    grad_up_w = dot32('td,tf->df', x_tokens, grad_up)
    grad_down_w = dot32('tf,td->fd', hidden, dy_tokens)
    grad_input = dot32('tf,df->td', grad_gate, shared_gate) + dot32('tf,df->td', grad_up, shared_up)
    return grad_input, grad_gate_w, grad_up_w, grad_down_w


def solution(mesh):
    group = mesh.shape['ep']
    token_spec = P(('dp', 'ep'), None)
    expert_spec = P('ep', None, None)
    whole_spec = P(None, None)
    grad_spec = P(('dp', 'ep'), None, None)

    def local_backward(x_tokens, dy_tokens, expert_ids, gate_vals, slot_pos, w_gate, w_up, w_down, shared_gate, shared_up, shared_down):
        tok_count, top_k = expert_ids.shape
        local_experts, model_dim, expert_ff = w_gate.shape
        num_experts = local_experts * group
        capacity = (3 * tok_count * top_k + 2 * num_experts - 1) // (2 * num_experts)
        rows = (capacity + 15) // 16 * 16
        meta = jnp.concatenate([expert_ids.astype(F32), slot_pos.astype(F32), gate_vals], axis=1).T
        x_all = lax.all_gather(x_tokens, 'ep')
        dy_all = lax.all_gather(dy_tokens, 'ep')
        meta_all = lax.all_gather(meta, 'ep')
        ids_all, slot_all, gate_all = meta_all[:, :top_k], meta_all[:, top_k:2 * top_k], meta_all[:, 2 * top_k:]
        first = (lax.axis_index('ep') * local_experts).astype(F32)
        mine = first + jnp.arange(local_experts, dtype=F32)
        hit = (ids_all[:, None] == mine[None, :, None, None]) & (slot_all[:, None] >= 0)
        tok_slot = jnp.sum(jnp.where(hit, slot_all[:, None] + 1.0, 0.0), axis=2) - 1.0
        tok_gate = jnp.sum(jnp.where(hit, gate_all[:, None], 0.0), axis=2)
        pick = tok_slot[:, :, None, :] == jnp.arange(rows, dtype=F32)[None, None, :, None]
        row_gate = jnp.sum(jnp.where(pick, tok_gate[:, :, None, :], 0.0), axis=3)
        pick = pick.astype(BF16)
        x_exp = dot32('sert,std->esrd', pick, x_all).astype(BF16).reshape(local_experts, group * rows, model_dim)
        dz_exp = (dot32('sert,std->esrd', pick, dy_all) * row_gate.transpose(1, 0, 2)[..., None]).astype(BF16).reshape(local_experts, group * rows, model_dim)
        act_gate = dot32('erd,edf->erf', x_exp, w_gate).astype(BF16)
        act_up = dot32('erd,edf->erf', x_exp, w_up).astype(BF16)
        grad_hidden = dot32('erd,efd->erf', dz_exp, w_down)
        hidden, grad_gate, grad_up = swiglu_parts(act_gate, act_up, grad_hidden)
        grad_exp = (dot32('erf,edf->erd', grad_gate, w_gate) + dot32('erf,edf->erd', grad_up, w_up)).astype(BF16)
        partial = dot32('sert,esrd->std', pick, grad_exp.reshape(local_experts, group, rows, model_dim))
        routed_sum = lax.psum_scatter(partial, 'ep', scatter_dimension=0, tiled=True)[0]
        grad_w_gate = dot32('erd,erf->edf', x_exp, grad_gate)
        grad_w_up = dot32('erd,erf->edf', x_exp, grad_up)
        grad_w_down = dot32('erf,erd->efd', hidden, dz_exp)
        shared_dx, grad_shared_gate, grad_shared_up, grad_shared_down = shared_backward(x_tokens, dy_tokens, shared_gate, shared_up, shared_down)
        grad_x = (routed_sum + shared_dx).astype(BF16)
        return grad_x, grad_w_gate, grad_w_up, grad_w_down, grad_shared_gate[None], grad_shared_up[None], grad_shared_down[None]

    return jax.shard_map(local_backward, mesh=mesh, in_specs=(token_spec, token_spec, token_spec, token_spec, token_spec, expert_spec, expert_spec, expert_spec, whole_spec, whole_spec, whole_spec), out_specs=(token_spec, grad_spec, grad_spec, grad_spec, grad_spec, grad_spec, grad_spec), check_vma=False)
```

time: 727 us -> 417 us (0.57)
  the two profiles are of different devices: /device:TPU:15 before, /device:TPU:0 now
where the time goes in v1:
time: 417 us; the launch traced here: 411 us
  waiting for transfers between devices  206 us (49%)
  matrix products  133 us (32%)
  local copies, waits for them, and re-layouts  30.3 us (7%)
  blocking collectives  24.5 us (6%)
  between operations  14.2 us (3%)
    dot_general x19, matrix products, dot32(): return jnp.einsum(spec, a, b, preferred_element_type=F32)  133 us
    reduce_scatter x1, waiting for transfers between devices, local_backward(): lax.psum_scatter(partial, 'ep', scatter_dimension=0, tiled=True)[0]  112 us
    all_gather x1, waiting for transfers between devices, local_backward(): x_all = lax.all_gather(x_tokens, 'ep')  51.9 us
    all_gather x1, waiting for transfers between devices, local_backward(): dy_all = lax.all_gather(dy_tokens, 'ep')  41.1 us
    all_gather x1, blocking collectives, local_backward(): meta_all = lax.all_gather(meta, 'ep')  24.5 us
    unnamed x34, local copies, waits for them, and re-layouts  13.3 us
    convert_element_type x1, local copies, waits for them, and re-layouts, local_backward(): (dot32('sert,std->esrd', pick, dy_all) * row_gate.transpose(1, 0, 2)[...,...  8.59 us
  transfers between devices with their start and end apart: 3, of which 3 were waited for; matrix products, arithmetic and copies ran while one was open for 23% of the time, Pallas kernels for 0%

profile of v1, /device:TPU:0, one launch (start us, length us, event | category | flops | bytes accessed | tf_op | source)
XLA Modules:
  0.0 411.2 jit_solution(18257089983114839554)
XLA Ops:
  10.8 24.5 %all-gather.3 = f32[16,30,128]{2,1,0:T(8,128)S(1)} all-gather(f32[1,30,128]{2,1,0:T(8,128)S(1)} %maximum_bitcast_fusion), channel_id=2, replica_groups=mesh['dp'=2,'ep'=16] {'ep'}, dimensions={0}, use_global_device_ids=true | all-gather | bytes 261120 | tf_op jit(solution)/shard_map/all_gather | solution.py:53
  36.1 51.9 %all-gather.9.cloned.1.call-done = bf16[2048,2048]{1,0:T(8,128)(2,1)} async-done(((bf16[128,2048]{1,0:T(8,128)(2,1)}), bf16[2048,2048]{1,0:T(8,128)(2,1)}) %all-gather.9.cloned.1.call-update) | async-done | bytes 8388624 | tf_op jit(solution)/shard_map/all_gather | solution.py:51
  88.0 9.1 %convert_bitcast_fusion = bf16[2,16,64,2048]{3,2,0,1:T(8,128)(2,1)} fusion(bf16[16,128,2048,1]{2,1,3,0:T(8,128)(2,1)} %bitcast.70, f32[16,2,128]{2,1,0:T(2,128)S(1)} %copy.56), kind=kOutput, calls=%fused_computation.5 | convolution fusion | flops 1078198272 | bytes 16793600 | tf_op jit(solution)/shard_map/sert,std->esrd/dot_general | solution.py:22
  97.1 8.3 %copy.60 = bf16[2,16,64,2048]{3,2,1,0:T(8,128)(2,1)} copy(bf16[2,16,64,2048]{3,2,0,1:T(8,128)(2,1)} %convert_bitcast_fusion) | data formatting | bytes 16777216 | tf_op jit(solution)/shard_map/convert_element_type | solution.py:63
  105.4 10.5 %convolution_convert_fusion.1 = bf16[2,1024,512]{2,1,0:T(8,128)(2,1)} fusion(bf16[2,1024,2048]{2,1,0:T(8,128)(2,1)} %bitcast.72, bf16[2,2048,512]{2,1,0:T(8,128)(2,1)} %param.17), kind=kOutput, calls=%fused_computation.29 | convolution fusion | flops 4296015872 | bytes 14680064 | tf_op jit(solution)/shard_map/erd,edf->erf/dot_general | solution.py:22
  115.9 5.9 %convolution_convert_fusion = bf16[2,1024,512]{2,1,0:T(8,128)(2,1)} fusion(bf16[2,1024,2048]{2,1,0:T(8,128)(2,1)S(1)} %bitcast.75, bf16[2,2048,512]{2,1,0:T(8,128)(2,1)S(1)} %copy-done.9), kind=kOutput, calls=%fused_computation.28 | convolution fusion | flops 4296015872 | bytes 14680064 | tf_op jit(solution)/shard_map/erd,edf->erf/dot_general | solution.py:22
  121.9 41.1 %all-gather.7.cloned.1.call-done = bf16[2048,2048]{1,0:T(8,128)(2,1)} async-done(((bf16[128,2048]{1,0:T(8,128)(2,1)}), bf16[2048,2048]{1,0:T(8,128)(2,1)}) %all-gather.7.cloned.1.call-update) | async-done | bytes 8388624 | tf_op jit(solution)/shard_map/all_gather | solution.py:52
  162.9 9.1 %fusion = bf16[2,16,64,2048]{3,2,0,1:T(8,128)(2,1)} fusion(f32[2,16,64]{2,0,1:T(2,128)S(1)} %bitcast.80, bf16[16,128,2048,1]{2,1,3,0:T(8,128)(2,1)} %bitcast.69, f32[16,2,128]{2,1,0:T(2,128)S(1)} %copy.56), kind=kOutput, calls=%fused_computation.1 | convolution fusion | flops 1082392576 | bytes 16801792 | tf_op jit(solution)/shard_map/sert,std->esrd/dot_general | solution.py:22
  172.0 8.6 %copy.59 = bf16[2,16,64,2048]{3,2,1,0:T(8,128)(2,1)} copy(bf16[2,16,64,2048]{3,2,0,1:T(8,128)(2,1)} %fusion) | data formatting | bytes 16777216 | tf_op jit(solution)/shard_map/convert_element_type | solution.py:64
  180.6 12.9 %fusion.8 = (bf16[2,1024,512]{2,1,0:T(8,128)(2,1)S(1)}, f32[2,1024,512]{2,1,0:T(8,128)}) fusion(bf16[2,1024,512]{2,1,0:T(8,128)(2,1)} %convolution_convert_fusion.1, bf16[2,1024,512]{2,1,0:T(8,128)(2,1)S(1)} %copy-done.13, bf16[2,1024,2048]{2,1,0:T(8,128)(2,1)} %bitcast.76, bf16[2,512,2048]{2,1,0:T(8,128)(2,1)} %param.18), kind=kOutput, calls=%fused_computation.14 | convolution fusion | flops 4307550208 | bytes 23068672 | tf_op jit(solution)/shard_map/erd,efd->erf/dot_general | solution.py:22
  193.6 8.1 %fusion.29 = f32[2,1024,2048]{2,1,0:T(8,128)} fusion(bf16[2,1024,512]{2,1,0:T(8,128)(2,1)S(1)} %get-tuple-element.49, bf16[2,2048,512]{2,1,0:T(8,128)(2,1)S(1)} %copy-done.10), kind=kOutput, calls=%fused_computation.56 | convolution fusion | flops 4294967296 | bytes 23068672 | tf_op jit(solution)/shard_map/erf,edf->erd/dot_general | solution.py:22
  201.7 13.8 %add_convert_fusion = bf16[2,1024,2048]{2,1,0:T(8,128)(2,1)} fusion(f32[2,1024,2048]{2,1,0:T(8,128)} %fusion.29, bf16[2,2048,512]{2,1,0:T(8,128)(2,1)} %param.17, f32[2,1024,512]{2,1,0:T(8,128)} %get-tuple-element.50, bf16[2,1024,512]{2,1,0:T(8,128)(2,1)} %convolution_convert_fusion), kind=kOutput, calls=%fused_computation.2 | convolution fusion | flops 4310695936 | bytes 35651584 | tf_op jit(solution)/shard_map/erf,edf->erd/dot_general | solution.py:22
  215.5 11.5 %fusion.3 = f32[16,128,2048]{2,1,0:T(8,128)} fusion(bf16[2,16,64,2048]{3,2,1,0:T(8,128)(2,1)} %bitcast.71, f32[16,2,128]{2,1,0:T(2,128)S(1)} %copy.56), kind=kOutput, calls=%fused_computation.6 | convolution fusion | flops 1074003968 | bytes 25182208 | tf_op jit(solution)/shard_map/sert,esrd->std/dot_general | solution.py:22
  228.5 2.3 fusion.19
  233.0 2.7 convolution_bitcast_fusion.2
  235.8 5.3 %copy.65 = f32[1,2048,512]{2,1,0:T(8,128)} copy(f32[1,2048,512]{1,2,0:T(8,128)} %convolution_bitcast_fusion.2) | data formatting | bytes 8388608
  241.1 2.7 convolution_bitcast_fusion.1
  243.8 5.5 %copy.66 = f32[1,2048,512]{2,1,0:T(8,128)} copy(f32[1,2048,512]{1,2,0:T(8,128)} %convolution_bitcast_fusion.1) | data formatting | bytes 8388608
  249.4 2.8 convolution_bitcast_fusion
  254.0 12.1 %fusion.31 = f32[2,2048,512]{2,1,0:T(8,128)} fusion(bf16[2,1024,2048]{2,1,0:T(8,128)(2,1)} %bitcast.73, bf16[2,1024,512]{2,1,0:T(8,128)(2,1)} %copy-done.12), kind=kOutput, calls=%fused_computation.58 | convolution fusion | flops 4294967296 | bytes 18874368 | tf_op jit(solution)/shard_map/erd,erf->edf/dot_general | solution.py:22
  266.1 9.7 %fusion.16 = f32[2,512,2048]{2,1,0:T(8,128)} fusion(bf16[2,1024,2048]{2,1,0:T(8,128)(2,1)S(1)} %bitcast.79, bf16[2,1024,512]{2,1,0:T(8,128)(2,1)} %convolution_convert_fusion.1, bf16[2,1024,512]{2,1,0:T(8,128)(2,1)} %convolution_convert_fusion), kind=kOutput, calls=%fused_computation.27 | convolution fusion | flops 4303355904 | bytes 20971520 | tf_op jit(solution)/shard_map/erf,erd->efd/dot_general | solution.py:22
  275.9 13.4 %fusion.27 = f32[2,2048,512]{2,1,0:T(8,128)} fusion(bf16[2,1024,2048]{2,1,0:T(8,128)(2,1)} %bitcast.74, f32[2,1024,512]{2,1,0:T(8,128)} %get-tuple-element.50, bf16[2,1024,512]{2,1,0:T(8,128)(2,1)} %convolution_convert_fusion), kind=kOutput, calls=%fused_computation.54 | convolution fusion | flops 4302307328 | bytes 23068672 | tf_op jit(solution)/shard_map/erd,erf->edf/dot_general | solution.py:22
  289.3 111.7 %reduce-scatter.2.cloned.1.call-done = f32[1,128,2048]{2,1,0:T(8,128)} async-done(((f32[16,128,2048]{2,1,0:T(8,128)}), f32[1,128,2048]{2,1,0:T(8,128)}) %reduce-scatter.2.cloned.1.call-update) | async-done | bytes 1048592 | tf_op jit(solution)/shard_map/reduce_scatter | solution.py:71
  400.9 3.5 fusion.15
  (56 shorter events, 9.9 us)
Async XLA Ops:
  7.2 219.8 %copy-start = (bf16[2048,512]{1,0:T(8,128)(2,1)S(1)}, bf16[2048,512]{1,0:T(8,128)(2,1)}, u32[]{:S(2)}) copy-start(bf16[2048,512]{1,0:T(8,128)(2,1)} %param.19) | copy-start | bytes 6291460
  7.2 80.8 %all-gather.9.cloned.1.call-start = ((), (), s32[]{:S(2)}) async-start(), calls=%async_computation.3 | async-start | bytes 8912896 | tf_op jit(solution)/shard_map/all_gather | solution.py:51
  7.9 155.0 %all-gather.7.cloned.1.call-start = ((), (), s32[]{:S(2)}) async-start(), calls=%async_computation.2 | async-start | bytes 8912896 | tf_op jit(solution)/shard_map/all_gather | solution.py:52
  8.7 392.3 %reduce-scatter.2.cloned.1.call-start = ((), (), s32[]{:S(2)}) async-start(), calls=%async_computation.1 | async-start | bytes 17825792 | tf_op jit(solution)/shard_map/reduce_scatter | solution.py:71
  105.4 10.5 %copy-start.2 = (bf16[2,16,64,2048]{3,2,1,0:T(8,128)(2,1)S(1)}, bf16[2,16,64,2048]{3,2,1,0:T(8,128)(2,1)}, u32[]{:S(2)}) copy-start(bf16[2,16,64,2048]{3,2,1,0:T(8,128)(2,1)} %copy.60) | copy-start | bytes 25165828
  105.4 10.5 %copy-start.9 = (bf16[2,2048,512]{2,1,0:T(8,128)(2,1)S(1)}, bf16[2,2048,512]{2,1,0:T(8,128)(2,1)}, u32[]{:S(2)}) copy-start(bf16[2,2048,512]{2,1,0:T(8,128)(2,1)} %param.16) | copy-start | bytes 12582916
  172.0 8.6 %copy-start.13 = (bf16[2,1024,512]{2,1,0:T(8,128)(2,1)S(1)}, bf16[2,1024,512]{2,1,0:T(8,128)(2,1)}, u32[]{:S(2)}) copy-start(bf16[2,1024,512]{2,1,0:T(8,128)(2,1)} %convolution_convert_fusion) | copy-start | bytes 6291460
  180.6 13.0 %copy-start.10 = (bf16[2,2048,512]{2,1,0:T(8,128)(2,1)S(1)}, bf16[2,2048,512]{2,1,0:T(8,128)(2,1)}, u32[]{:S(2)}) copy-start(bf16[2,2048,512]{2,1,0:T(8,128)(2,1)} %param.16) | copy-start | bytes 12582916
  193.6 8.1 %copy-start.12 = (bf16[2,1024,512]{2,1,0:T(8,128)(2,1)}, bf16[2,1024,512]{2,1,0:T(8,128)(2,1)S(1)}, u32[]{:S(2)}) copy-start(bf16[2,1024,512]{2,1,0:T(8,128)(2,1)S(1)} %get-tuple-element.49) | copy-start | bytes 6291460
  227.0 1.0 copy-start.1
  228.0 3.4 copy-start.4
  228.0 3.4 copy-start.11
  230.8 0.7 copy-start.5
  232.4 0.7 copy-start.7
  243.8 5.5 %copy-start.6 = (f32[128,512]{1,0:T(8,128)S(1)}, f32[128,512]{1,0:T(8,128)}, u32[]{:S(2)}) copy-start(f32[128,512]{1,0:T(8,128)} %copy-done.5) | copy-start | bytes 786436
  249.4 2.8 copy-start.8
  252.2 13.9 %slice-start = ((s8[8388608]{0:T(1024)(128)(4,1)}), s8[4194304]{0:T(1024)(128)(4,1)S(1)}, s32[]{:S(2)}) async-start(s8[8388608]{0:T(1024)(128)(4,1)} %bitcast.77), calls=%async_computation.4 | async-start | bytes 8388608
  254.0 12.1 %slice-start.1 = ((s8[8388608]{0:T(1024)(128)(4,1)}), s8[4194304]{0:T(1024)(128)(4,1)S(1)}, s32[]{:S(2)}) async-start(s8[8388608]{0:T(1024)(128)(4,1)} %bitcast.77), calls=%async_computation.5 | async-start | bytes 8388608
  275.8 125.1 %copy-start.3 = (f32[128,2048]{1,0:T(8,128)S(1)}, f32[128,2048]{1,0:T(8,128)}, u32[]{:S(2)}) copy-start(f32[128,2048]{1,0:T(8,128)} %fusion.30) | copy-start | bytes 3145732
Sparse Core Ops, SparseCore 0:
  10.2 77.8 all-gather.8
  90.2 72.7 all-gather.6
  227.1 173.7 reduce-scatter.1

commit v2 on v1

v2 whole, which is shorter than its diff:
```python
import functools

import jax
import jax.numpy as jnp
from jax import lax
from jax.experimental import pallas as pl
from jax.experimental.pallas import tpu as pltpu
from jax.sharding import PartitionSpec as P

F32 = jnp.float32
BF16 = jnp.bfloat16
ANY = pl.BlockSpec(memory_space=pl.ANY)
VMEM = pl.BlockSpec(memory_space=pltpu.VMEM)
VMEM_LIMIT = 67_000_000


def dot_nn(a, b):
    return lax.dot_general(a, b, (((1,), (0,)), ((), ())), preferred_element_type=F32)


def dot_nt(a, b):
    return lax.dot_general(a, b, (((1,), (1,)), ((), ())), preferred_element_type=F32)


def dot_tn(a, b):
    return lax.dot_general(a, b, (((0,), (0,)), ((), ())), preferred_element_type=F32)


def swiglu_parts(act_gate, act_up, grad_hidden):
    gate_f32 = act_gate.astype(F32)
    up_f32 = act_up.astype(F32)
    sigma = jax.nn.sigmoid(gate_f32)
    silu_gate = gate_f32 * sigma
    hidden = (silu_gate * up_f32).astype(BF16)
    grad_gate = (grad_hidden * up_f32 * sigma * (1.0 + gate_f32 * (1.0 - sigma))).astype(BF16)
    grad_up = (grad_hidden * silu_gate).astype(BF16)
    return hidden, grad_gate, grad_up


def routed_kernel(x_in, dy_in, gate_tab, w_gate, w_up, w_down,
                  routed_out, x_all, z_all, act_all, hid_all,
                  xbuf, dybuf, gbuf, w13, w2, act, hst, zst,
                  sums, dsend, pbuf, ybuf, cbuf,
                  load_sem, out_sem, gs_sem, gr_sem, recv_sem, sy_sem, sd_sem, sown_sem, sz_sem,
                  ds_sem, dr_sem, ys_sem, yr_sem, cs_sem, cr_sem, credit):
    tok, dim = x_in.shape
    ff = w2.shape[1]
    me = lax.axis_index('ep')
    z = lax.div(me, 4)
    y = lax.rem(lax.div(me, 2), 2)
    c = lax.rem(me, 2)
    partner = me + 1 - 2 * c
    side = me + 2 - 4 * y
    bufs = (xbuf, dybuf)

    def bid(zz, yy, cc):
        return zz * 4 + yy * 2 + cc

    def order(k):
        near = lax.div(z * (3 - z), 2)
        flip = lax.div(z, 2)
        delta = lax.div((1 - k) * (2 - k) * (3 - k), 6) - lax.div(k * (2 - k) * (3 - k), 2)
        base = k + near * delta
        return base + flip * (3 - 2 * base)

    def visit(t):
        u = t + lax.div(t, 7)
        odd = lax.rem(u, 2)
        first = lax.div(7 - t, 7)
        k = odd * lax.div(u + 1, 2) + (1 - odd) * (lax.div(u, 2) - 1) + first
        col = 1 - odd - first
        return order(k), y + col * (1 - 2 * y), col

    def remote(src, dst, send, recv, dev):
        return pltpu.make_async_remote_copy(src_ref=src, dst_ref=dst, send_sem=send, recv_sem=recv, device_id={'ep': dev}, device_id_type=pl.DeviceIdType.MESH)

    own = [pltpu.make_async_copy(x_in, xbuf.at[me], load_sem.at[0]), pltpu.make_async_copy(dy_in, dybuf.at[me], load_sem.at[1])]
    loads = []
    for e in range(2):
        loads.append(pltpu.make_async_copy(w_gate.at[e], w13.at[e, :, pl.ds(0, ff)], load_sem.at[2 + 3 * e]))
        loads.append(pltpu.make_async_copy(w_up.at[e], w13.at[e, :, pl.ds(ff, ff)], load_sem.at[3 + 3 * e]))
        loads.append(pltpu.make_async_copy(w_down.at[e], w2.at[e], load_sem.at[4 + 3 * e]))
    for cp in own + loads:
        cp.start()

    barrier = pltpu.get_barrier_semaphore()

    @pl.loop(1, 16)
    def _(d):
        pl.semaphore_signal(barrier, inc=1, device_id={'ep': lax.rem(me + d, 16)}, device_id_type=pl.DeviceIdType.MESH)
    pl.semaphore_wait(barrier, 15)

    def send_y(q, zb, b):
        return remote(bufs[q].at[b], bufs[q].at[b], sy_sem.at[q, zb], recv_sem.at[q, b], side)

    def send_d(q, zb, yb, b):
        return remote(bufs[q].at[b], bufs[q].at[b], sd_sem.at[q, zb * 2 + yb], recv_sem.at[q, b], partner)

    def send_own(q, up):
        return remote(bufs[q].at[me], bufs[q].at[me], sown_sem.at[q, up], recv_sem.at[q, me], me + (4 if up else -4))

    def send_fwd(q, zb, b, up):
        return remote(bufs[q].at[b], bufs[q].at[b], sz_sem.at[q, zb], recv_sem.at[q, b], me + (4 if up else -4))

    for q in range(2):
        own[q].wait()
        send_y(q, z, me).start()

        @pl.when(z < 3)
        def _():
            send_own(q, 1).start()

        @pl.when(z > 0)
        def _():
            send_own(q, 0).start()
        send_d(q, z, y, me).start()

    def send_gate(d):
        dest = lax.rem(me + d, 16)
        return remote(gate_tab.at[dest], gbuf.at[me], gs_sem.at[d], gr_sem.at[me], dest)

    @pl.loop(1, 16)
    def _(d):
        send_gate(d).start()
    gbuf[me] = gate_tab[me]

    def arrive(t):
        zb, yb, col = visit(t)
        b = bid(zb, yb, c)
        for q in range(2):
            send_d(q, zb, yb, b).wait_recv()

            @pl.when(col == 0)
            def _():
                send_y(q, zb, b).start()

                @pl.when((zb > z) & (z > 0))
                def _():
                    send_fwd(q, zb, b, 0).start()

                @pl.when((zb < z) & (z < 3))
                def _():
                    send_fwd(q, zb, b, 1).start()
            send_d(q, zb, yb, b).start()

    def flush(t, start):
        zb, yb, _ = visit(t)
        b0 = bid(zb, yb, 0)
        two = pl.ds(b0, 2)
        cps = [pltpu.make_async_copy(xbuf.at[two], x_all.at[two], out_sem.at[0, t]),
               pltpu.make_async_copy(act.at[two], act_all.at[two], out_sem.at[1, t]),
               pltpu.make_async_copy(hst, hid_all.at[two], out_sem.at[2, t]),
               pltpu.make_async_copy(zst.at[0], z_all.at[0, two], out_sem.at[3, t]),
               pltpu.make_async_copy(zst.at[1], z_all.at[1, two], out_sem.at[4, t])]
        for cp in (cps if start else cps[2:]):
            if start:
                cp.start()
            else:
                cp.wait()

    def compute(t):
        zb, yb, _ = visit(t)
        b0 = bid(zb, yb, 0)
        bp = bid(zb, yb, 1 - c)
        for q in range(2):
            send_d(q, zb, yb, bp).wait_recv()
        for p in range(2):
            @pl.when(b0 + p != me)
            def _():
                remote(gate_tab.at[0], gbuf.at[b0 + p], gs_sem.at[0], gr_sem.at[b0 + p], partner).wait_recv()

        @pl.when(t > 0)
        def _():
            flush(t - 1, False)
        two = pl.ds(b0, 2)
        gates = jnp.concatenate([gbuf[b0].T, gbuf[b0 + 1].T], axis=0)
        for e in range(2):
            gate = gates[:, e:e + 1]
            zst[e] = (dybuf[two].reshape(2 * tok, dim).astype(F32) * gate).astype(BF16).reshape(2, tok, dim)
            ab = jnp.where(gate != 0.0, dot_nn(xbuf[two].reshape(2 * tok, dim), w13[e]), 0.0).astype(BF16)
            grad_hidden = dot_nt(zst[e].reshape(2 * tok, dim), w2[e])
            hidden, grad_gate, grad_up = swiglu_parts(ab[:, :ff], ab[:, ff:], grad_hidden)
            hst[:, :, e * ff:(e + 1) * ff] = hidden.reshape(2, tok, ff)
            act[two, :, 2 * e * ff:(2 * e + 1) * ff] = grad_gate.reshape(2, tok, ff)
            act[two, :, (2 * e + 1) * ff:(2 * e + 2) * ff] = grad_up.reshape(2, tok, ff)
        flush(t, True)

    for i, cp in enumerate(loads):
        cp.wait()

    @pl.loop(1, 9)
    def _(t):
        @pl.when(t < 8)
        def _():
            arrive(t)
        compute(t - 1)

    def rs_visit(j):
        half = lax.div(j, 4)
        zb = order(3 - lax.rem(j, 4))
        col = 1 - half
        return zb, y + col * (1 - 2 * y)

    def give(j):
        return remote(dsend.at[lax.rem(j, 2)], pbuf.at[lax.rem(j, 2)], ds_sem.at[lax.rem(j, 2)], dr_sem.at[lax.rem(j, 2)], partner)

    def rs_y(j):
        zb, _ = rs_visit(j)
        return remote(sums.at[j], ybuf.at[zb], ys_sem.at[zb], yr_sem.at[zb], side)

    tile = min(512, dim)

    def rs_compute(j):
        zb, yb = rs_visit(j)
        b = bid(zb, yb, c)
        bp = bid(zb, yb, 1 - c)

        @pl.when(j >= 2)
        def _():
            give(j).wait_send()

        @pl.loop(0, dim // tile)
        def _(n):
            cols = pl.ds(pl.multiple_of(n * tile, tile), tile)
            part = None
            for e in range(2):
                lanes = slice(2 * e * ff, (2 * e + 2) * ff)
                rows = jnp.concatenate([act[b, :, lanes], act[bp, :, lanes]], axis=0)
                r = dot_nt(rows, w13[e, cols, :]).astype(BF16).astype(F32)
                part = r if part is None else part + r
            sums[j, :, cols] = part[:tok]
            dsend[lax.rem(j, 2), :, cols] = part[tok:]

        @pl.when(j >= 2)
        def _():
            pl.semaphore_wait(credit, 1)
        give(j).start()

    def rs_finish(j):
        give(j).wait_recv()
        sums[j] = sums[j] + pbuf[lax.rem(j, 2)]

        @pl.when(j < 6)
        def _():
            pl.semaphore_signal(credit, inc=1, device_id={'ep': partner}, device_id_type=pl.DeviceIdType.MESH)

        @pl.when(j < 4)
        def _():
            rs_y(j).start()

    @pl.loop(0, 9)
    def _(j):
        @pl.when(j < 8)
        def _():
            rs_compute(j)

        @pl.when(j > 0)
        def _():
            rs_finish(j - 1)

    def chain(k, zb, up):
        j = 7 - k
        if up:
            return remote(sums.at[j], cbuf.at[0, zb - z - 1], cs_sem.at[k], cr_sem.at[0, zb - z - 1], me + 4)
        return remote(sums.at[j], cbuf.at[1, z - zb - 1], cs_sem.at[k], cr_sem.at[1, z - zb - 1], me - 4)

    def chain_in(j, up, gap):
        slot = 0 if up else 1
        remote(sums.at[j], cbuf.at[slot, gap], cs_sem.at[0], cr_sem.at[slot, gap], partner).wait_recv()
        sums[j] = sums[j] + cbuf[slot, gap]

    for k in (3, 2, 1, 0):
        zb = order(k)
        j = 7 - k
        remote(sums.at[j], ybuf.at[zb], ys_sem.at[zb], yr_sem.at[zb], side).wait_recv()
        sums[j] = sums[j] + ybuf[zb]
        if k:
            @pl.when(zb > z)
            def _():
                @pl.when(z > 0)
                def _():
                    chain_in(j, True, zb - z)
                chain(k, zb, True).start()

            @pl.when(zb < z)
            def _():
                @pl.when(z < 3)
                def _():
                    chain_in(j, False, z - zb)
                chain(k, zb, False).start()
        else:
            @pl.when(z > 0)
            def _():
                chain_in(7, True, 0)

            @pl.when(z < 3)
            def _():
                chain_in(7, False, 0)
            done = pltpu.make_async_copy(sums.at[7], routed_out, load_sem.at[0])
            done.start()

    done.wait()
    flush(7, False)
    for t in range(8):
        for i, ref in enumerate((xbuf, act)):
            pltpu.make_async_copy(ref.at[pl.ds(0, 2)], (x_all, act_all)[i].at[pl.ds(0, 2)], out_sem.at[i, t]).wait()
    for q in range(2):
        for zb in range(4):
            send_y(q, zb, 0).wait_send()
            for yb in range(2):
                send_d(q, zb, yb, 0).wait_send()

            @pl.when(((zb > z) & (z > 0)) | ((zb < z) & (z < 3)))
            def _():
                send_fwd(q, zb, 0, 1).wait_send()

        @pl.when(z < 3)
        def _():
            send_own(q, 1).wait_send()

        @pl.when(z > 0)
        def _():
            send_own(q, 0).wait_send()

    @pl.loop(1, 16)
    def _(d):
        send_gate(d).wait_send()
    for j in range(2):
        give(j).wait_send()
    for j in range(4):
        remote(sums.at[j], ybuf.at[j], ys_sem.at[j], yr_sem.at[j], side).wait_send()
    for k in range(1, 4):
        remote(sums.at[0], cbuf.at[0, 0], cs_sem.at[k], cr_sem.at[0, 0], partner).wait_send()


def routed(x_tokens, dy_tokens, gate_tab, w_gate, w_up, w_down):
    tok, dim = x_tokens.shape
    ff = w_gate.shape[2]
    dma = pltpu.SemaphoreType.DMA
    flops = 16 * tok * 2 * 2 * dim * ff * 5
    return pl.pallas_call(
        routed_kernel,
        name='routed',
        out_shape=(jax.ShapeDtypeStruct((tok, dim), F32), jax.ShapeDtypeStruct((16, tok, dim), BF16), jax.ShapeDtypeStruct((2, 16, tok, dim), BF16),
                   jax.ShapeDtypeStruct((16, tok, 4 * ff), BF16), jax.ShapeDtypeStruct((16, tok, 2 * ff), BF16)),
        in_specs=[ANY, ANY, VMEM, ANY, ANY, ANY],
        out_specs=(ANY,) * 5,
        scratch_shapes=[
            pltpu.VMEM((16, tok, dim), BF16), pltpu.VMEM((16, tok, dim), BF16), pltpu.VMEM((16, 8, tok), F32),
            pltpu.VMEM((2, dim, 2 * ff), BF16), pltpu.VMEM((2, ff, dim), BF16),
            pltpu.VMEM((16, tok, 4 * ff), BF16), pltpu.VMEM((2, tok, 2 * ff), BF16), pltpu.VMEM((2, 2, tok, dim), BF16),
            pltpu.VMEM((8, tok, dim), F32), pltpu.VMEM((2, tok, dim), F32), pltpu.VMEM((2, tok, dim), F32),
            pltpu.VMEM((4, tok, dim), F32), pltpu.VMEM((2, 3, tok, dim), F32),
            dma((8,)), dma((5, 8)), dma((16,)), dma((16,)), dma((2, 16)), dma((2, 4)), dma((2, 8)), dma((2, 2)), dma((2, 4)),
            dma((2,)), dma((2,)), dma((4,)), dma((4,)), dma((4,)), dma((2, 3)), pltpu.SemaphoreType.REGULAR,
        ],
        compiler_params=pltpu.CompilerParams(collective_id=0, has_side_effects=True, vmem_limit_bytes=VMEM_LIMIT),
        cost_estimate=pl.CostEstimate(flops=flops, bytes_accessed=80_000_000, transcendentals=0),
    )(x_tokens, dy_tokens, gate_tab, w_gate, w_up, w_down)


def shared_kernel(x, dy, w1, w3, w2, dx, g1, g3, g2):
    act_gate = dot_nn(x[...], w1[...]).astype(BF16)
    act_up = dot_nn(x[...], w3[...]).astype(BF16)
    grad_hidden = dot_nt(dy[...], w2[...])
    hidden, grad_gate, grad_up = swiglu_parts(act_gate, act_up, grad_hidden)
    dx[...] = dot_nt(grad_gate, w1[...]) + dot_nt(grad_up, w3[...])
    g1[0] = dot_tn(x[...], grad_gate)
    g3[0] = dot_tn(x[...], grad_up)
    g2[0] = dot_tn(hidden, dy[...])


def shared_backward(x, dy, w1, w3, w2):
    tok, dim = x.shape
    ff = w1.shape[1]
    return pl.pallas_call(
        shared_kernel,
        name='shared',
        out_shape=(jax.ShapeDtypeStruct((tok, dim), F32), jax.ShapeDtypeStruct((1, dim, ff), F32), jax.ShapeDtypeStruct((1, dim, ff), F32), jax.ShapeDtypeStruct((1, ff, dim), F32)),
        in_specs=[VMEM] * 5,
        out_specs=(VMEM,) * 4,
        compiler_params=pltpu.CompilerParams(vmem_limit_bytes=60_000_000),
        cost_estimate=pl.CostEstimate(flops=16 * tok * dim * ff, bytes_accessed=21_000_000, transcendentals=tok * ff),
    )(x, dy, w1, w3, w2)


def up_grad_kernel(x, act, g1, g3):
    ff = act.shape[1] // 2
    both = dot_tn(x[...], act[...])
    g1[0] = both[:, :ff]
    g3[0] = both[:, ff:]


def up_grads(x_all, act_all):
    rows, dim = x_all.shape
    ff = act_all.shape[1] // 4
    tile = min(512, dim)
    out = jax.ShapeDtypeStruct((2, dim, ff), F32)
    return pl.pallas_call(
        up_grad_kernel,
        name='up_grads',
        out_shape=(out, out),
        grid=(dim // tile, 2),
        in_specs=[pl.BlockSpec((rows, tile), lambda i, e: (0, i)), pl.BlockSpec((rows, 2 * ff), lambda i, e: (0, e))],
        out_specs=(pl.BlockSpec((1, tile, ff), lambda i, e: (e, i, 0)), pl.BlockSpec((1, tile, ff), lambda i, e: (e, i, 0))),
        compiler_params=pltpu.CompilerParams(vmem_limit_bytes=60_000_000),
        cost_estimate=pl.CostEstimate(flops=8 * rows * dim * ff, bytes_accessed=50_000_000, transcendentals=0),
    )(x_all, act_all)


def down_grad_kernel(hid, dz, g2):
    g2[0] = dot_tn(hid[...], dz[0])


def down_grads(hid_all, z_all):
    _, rows, dim = z_all.shape
    ff = hid_all.shape[1] // 2
    tile = min(512, dim)
    return pl.pallas_call(
        down_grad_kernel,
        name='down_grads',
        out_shape=jax.ShapeDtypeStruct((2, ff, dim), F32),
        grid=(2, dim // tile),
        in_specs=[pl.BlockSpec((rows, ff), lambda e, n: (0, e)), pl.BlockSpec((1, rows, tile), lambda e, n: (e, 0, n))],
        out_specs=pl.BlockSpec((1, ff, tile), lambda e, n: (e, 0, n)),
        compiler_params=pltpu.CompilerParams(vmem_limit_bytes=60_000_000),
        cost_estimate=pl.CostEstimate(flops=4 * rows * dim * ff, bytes_accessed=30_000_000, transcendentals=0),
    )(hid_all, z_all)


def solution(mesh):
    group = mesh.shape['ep']
    token_spec = P(('dp', 'ep'), None)
    expert_spec = P('ep', None, None)
    whole_spec = P(None, None)
    grad_spec = P(('dp', 'ep'), None, None)

    def local_backward(x_tokens, dy_tokens, expert_ids, gate_vals, slot_pos, w_gate, w_up, w_down, shared_gate, shared_up, shared_down):
        tok, dim = x_tokens.shape
        local_experts = w_gate.shape[0]
        experts = jnp.arange(group * local_experts, dtype=jnp.int32)
        hit = (expert_ids.T[None] == experts[:, None, None]) & (slot_pos.T[None] >= 0)
        table = jnp.sum(jnp.where(hit, gate_vals.T[None], 0.0), axis=1)
        gate_tab = jnp.pad(table.reshape(group, local_experts, tok), ((0, 0), (0, 8 - local_experts), (0, 0)))
        shared_dx, grad_shared_gate, grad_shared_up, grad_shared_down = shared_backward(x_tokens, dy_tokens, shared_gate, shared_up, shared_down)
        routed_sum, x_all, z_all, act_all, hid_all = routed(x_tokens, dy_tokens, gate_tab, w_gate, w_up, w_down)
        rows = group * tok
        grad_w_gate, grad_w_up = up_grads(x_all.reshape(rows, dim), act_all.reshape(rows, -1))
        grad_w_down = down_grads(hid_all.reshape(rows, -1), z_all.reshape(local_experts, rows, dim))
        grad_x = (routed_sum + shared_dx).astype(BF16)
        return grad_x, grad_w_gate, grad_w_up, grad_w_down, grad_shared_gate, grad_shared_up, grad_shared_down

    return jax.shard_map(local_backward, mesh=mesh, in_specs=(token_spec, token_spec, token_spec, token_spec, token_spec, expert_spec, expert_spec, expert_spec, whole_spec, whole_spec, whole_spec), out_specs=(token_spec, grad_spec, grad_spec, grad_spec, grad_spec, grad_spec, grad_spec), check_vma=False)
```

time: 417 us -> 271 us (0.65); the launches traced: 411 us -> 271 us
  Pallas kernels: 0 us -> 266 us
  waiting for transfers between devices: 206 us -> 0 us
  matrix products: 133 us -> 0 us
  local copies, waits for them, and re-layouts: 30.3 us -> 0.64 us
  blocking collectives: 24.5 us -> 0 us
  between operations: 14.2 us -> 0.65 us
    pallas_call x0 -> x4, Pallas kernels: none -> 266 us  [the longest x1 210 us: routed(): pl.pallas_call(routed_kernel, name='routed', out_shape=(jax.ShapeDtypeStr...]
    dot_general x19 -> x0, matrix products: 133 us -> none  [dot32(): return jnp.einsum(spec, a, b, preferred_element_type=F32)]
    reduce_scatter x1 -> x0, waiting for transfers between devices: 112 us -> none  [local_backward(): lax.psum_scatter(partial, 'ep', scatter_dimension=0, tiled=True)[0]]
    all_gather x2 -> x0, waiting for transfers between devices: 93 us -> none  [the longest x1 51.9 us: local_backward(): x_all = lax.all_gather(x_tokens, 'ep')]
    all_gather x1 -> x0, blocking collectives: 24.5 us -> none  [local_backward(): meta_all = lax.all_gather(meta, 'ep')]
    convert_element_type x2 -> x0, local copies, waits for them, and re-layouts: 16.9 us -> none  [the longest x1 8.59 us: local_backward(): (dot32('sert,std->esrd', pick, dy_all) * row_gate.transpose(1, 0, 2)[...,...]
    unnamed x34 -> x2, local copies, waits for them, and re-layouts: 13.3 us -> 0.01 us
  transfers between devices with their start and end apart: 3 -> 0, of which waited for: 3 -> 0; matrix products, arithmetic and copies ran while one was open for 23% -> 0% of each run, Pallas kernels for 0% -> 0%
where the time goes in v2:
time: 271 us
  Pallas kernels  266 us (98%)
  other arithmetic  3.63 us (1%)
    pallas_call x1, Pallas kernels, routed(): pl.pallas_call(routed_kernel, name='routed', out_shape=(jax.ShapeDtypeStr...  210 us
    pallas_call x1, Pallas kernels, up_grads(): pl.pallas_call(up_grad_kernel, name='up_grads', out_shape=(out, out), gri...  27.6 us
    pallas_call x1, Pallas kernels, down_grads(): pl.pallas_call(down_grad_kernel, name='down_grads', out_shape=jax.ShapeDt...  16.7 us
    pallas_call x1, Pallas kernels, shared_backward(): pl.pallas_call(shared_kernel, name='shared', out_shape=(jax.ShapeDtypeStr...  11.3 us

profile of v2, /device:TPU:0, one launch (start us, length us, event | category | flops | bytes accessed | tf_op | source)
XLA Modules:
  0.0 270.8 jit_solution(13177382985892434102)
XLA Ops:
  0.6 0.7 compare_bitcast_fusion
  1.3 0.8 select_reduce_fusion
  2.1 0.6 pad.4.gate_tab
  2.7 210.3 %routed.1 = (f32[128,2048]{1,0:T(8,128)}, bf16[16,128,2048]{2,1,0:T(8,128)(2,1)}, bf16[2,16,128,2048]{3,2,1,0:T(8,128)(2,1)}, bf16[16,128,2048]{2,1,0:T(8,128)(2,1)}, bf16[16,128,1024]{2,1,0:T(8,128)(2,1)}) custom-call(bf16[128,2048]{1,0:T(8,128)(2,1)} %x.3, bf16[128,2048]{1,0:T(8,128)(2,1)} %dy.1, f32[16,8,128]{2,1,0:T(8,128)} %pad.4.gate_tab, ...), custom_call_target="tpu_custom_call" | custom-call | flops 42949672960 | bytes 80000000 | tf_op jit(solution)/shard_map/routed/pallas_call | solution.py:341
  213.0 27.6 %up_grads.1 = (f32[2,2048,512]{2,1,0:T(8,128)}, f32[2,2048,512]{2,1,0:T(8,128)}) custom-call(bf16[2048,2048]{1,0:T(8,128)(2,1)} %bitcast.13, bf16[2048,2048]{1,0:T(8,128)(2,1)} %bitcast.14), custom_call_target="tpu_custom_call" | custom-call | flops 17179869184 | bytes 50000000 | tf_op jit(solution)/shard_map/up_grads/pallas_call | solution.py:399
  240.6 16.7 %down_grads.1 = f32[2,512,2048]{2,1,0:T(8,128)} custom-call(bf16[2048,1024]{1,0:T(8,128)(2,1)} %bitcast.15, bf16[2,2048,2048]{2,1,0:T(8,128)(2,1)} %bitcast.12), custom_call_target="tpu_custom_call" | custom-call | flops 8589934592 | bytes 30000000 | tf_op jit(solution)/shard_map/down_grads/pallas_call | solution.py:419
  257.4 0.0 copy-start
  257.4 11.3 %shared.1 = (f32[128,2048]{1,0:T(8,128)}, f32[1,2048,512]{2,1,0:T(8,128)}, f32[1,2048,512]{2,1,0:T(8,128)}, f32[1,512,2048]{2,1,0:T(8,128)}) custom-call(bf16[128,2048]{1,0:T(8,128)(2,1)} %x.3, bf16[128,2048]{1,0:T(8,128)(2,1)} %dy.1, bf16[2048,512]{1,0:T(8,128)(2,1)} %w1.1, bf16[2048,512]{1,0:T(8,128)(2,1)} %w3.1, bf16[512,2048]{1,0:T(8,128)(2,1)} %w2.1), custom_call_target="tpu_custom_call" | custom-call | flops 2147483648 | bytes 21000000 | tf_op jit(solution)/shard_map/shared/pallas_call | solution.py:376
  268.6 0.0 copy-done
  268.6 2.2 add_convert_fusion
Async XLA Ops:
  257.4 11.3 %copy-start = (f32[128,2048]{1,0:T(8,128)S(1)}, f32[128,2048]{1,0:T(8,128)}, u32[]{:S(2)}) copy-start(f32[128,2048]{1,0:T(8,128)} %get-tuple-element.18) | copy-start | bytes 3145732

commit v3 on v2

v3 whole, which is shorter than its diff:
```python
import functools

import jax
import jax.numpy as jnp
from jax import lax
from jax.experimental import pallas as pl
from jax.experimental.pallas import tpu as pltpu
from jax.sharding import PartitionSpec as P

F32 = jnp.float32
BF16 = jnp.bfloat16
ANY = pl.BlockSpec(memory_space=pl.ANY)
VMEM = pl.BlockSpec(memory_space=pltpu.VMEM)
VMEM_LIMIT = 67_000_000


def dot_nn(a, b):
    return lax.dot_general(a, b, (((1,), (0,)), ((), ())), preferred_element_type=F32)


def dot_nt(a, b):
    return lax.dot_general(a, b, (((1,), (1,)), ((), ())), preferred_element_type=F32)


def dot_tn(a, b):
    return lax.dot_general(a, b, (((0,), (0,)), ((), ())), preferred_element_type=F32)


def swiglu_parts(act_gate, act_up, grad_hidden):
    gate_f32 = act_gate.astype(F32)
    up_f32 = act_up.astype(F32)
    sigma = jax.nn.sigmoid(gate_f32)
    silu_gate = gate_f32 * sigma
    hidden = (silu_gate * up_f32).astype(BF16)
    grad_gate = (grad_hidden * up_f32 * sigma * (1.0 + gate_f32 * (1.0 - sigma))).astype(BF16)
    grad_up = (grad_hidden * silu_gate).astype(BF16)
    return hidden, grad_gate, grad_up


def routed_kernel(x_in, dy_in, table, w_gate, w_up, w_down, s_gate, s_up, s_down,
                  grad_x, x_all, z_all, act_all, hid_all, sact_out, shid_out,
                  xbuf, dybuf, tbuf, pick, w13, w2, act, hst, xst, zst, sact, shid, sdx,
                  sums, dsend, pbuf, ybuf, cbuf, ebuf,
                  load_sem, out_sem, gs_sem, gr_sem, recv_sem, sy_sem, sd_sem, sown_sem, sz_sem, sx_sem,
                  ds_sem, dr_sem, ys_sem, yr_sem, cs_sem, cr_sem, es_sem, er_sem, credit):
    tok, dim = x_in.shape
    ff = w2.shape[1]
    cap = xst.shape[2]
    half = dim // 2
    tile = min(512, dim)
    me = lax.axis_index('ep')
    z = lax.div(me, 4)
    y = lax.rem(lax.div(me, 2), 2)
    c = lax.rem(me, 2)
    partner = me + 1 - 2 * c
    side = me + 2 - 4 * y
    inner = z * (3 - z)
    near_end = lax.div(z, 2)
    far_end = 1 - near_end
    bufs = (xbuf, dybuf)

    def bid(zz, yy, cc):
        return zz * 4 + yy * 2 + cc

    def order(k):
        near = lax.div(inner, 2)
        delta = lax.div((1 - k) * (2 - k) * (3 - k), 6) - lax.div(k * (2 - k) * (3 - k), 2)
        base = k + near * delta
        return base + near_end * (3 - 2 * base)

    def visit(t):
        u = t + lax.div(t, 7)
        odd = lax.rem(u, 2)
        first = lax.div(7 - t, 7)
        k = odd * lax.div(u + 1, 2) + (1 - odd) * (lax.div(u, 2) - 1) + first
        col = 1 - odd - first
        return order(k), y + col * (1 - 2 * y), col

    def remote(src, dst, send, recv, dev):
        return pltpu.make_async_remote_copy(src_ref=src, dst_ref=dst, send_sem=send, recv_sem=recv, device_id={'ep': dev}, device_id_type=pl.DeviceIdType.MESH)

    def weights(e, gate, up, down):
        return [pltpu.make_async_copy(gate, w13.at[e, :, pl.ds(0, ff)], load_sem.at[2 + 3 * e]),
                pltpu.make_async_copy(up, w13.at[e, :, pl.ds(ff, ff)], load_sem.at[3 + 3 * e]),
                pltpu.make_async_copy(down, w2.at[e], load_sem.at[4 + 3 * e])]

    own = [pltpu.make_async_copy(x_in, xbuf.at[me], load_sem.at[0]), pltpu.make_async_copy(dy_in, dybuf.at[me], load_sem.at[1])]
    shared_load = weights(1, s_gate, s_up, s_down)
    first_load = weights(0, w_gate.at[0], w_up.at[0], w_down.at[0])
    second_load = weights(1, w_gate.at[1], w_up.at[1], w_down.at[1])
    for cp in own + shared_load + first_load:
        cp.start()

    barrier = pltpu.get_barrier_semaphore()

    @pl.loop(1, 16)
    def _(d):
        pl.semaphore_signal(barrier, inc=1, device_id={'ep': lax.rem(me + d, 16)}, device_id_type=pl.DeviceIdType.MESH)
    pl.semaphore_wait(barrier, 15)

    def send_y(q, zb, b):
        return remote(bufs[q].at[b], bufs[q].at[b], sy_sem.at[q, zb], recv_sem.at[q, b], side)

    def send_d(q, zb, yb, b):
        return remote(bufs[q].at[b], bufs[q].at[b], sd_sem.at[q, zb * 2 + yb], recv_sem.at[q, b], partner)

    def send_own(q, up):
        return remote(bufs[q].at[me], bufs[q].at[me], sown_sem.at[q, up], recv_sem.at[q, me], me + (4 if up else -4))

    def send_fwd(q, zb, b, up):
        return remote(bufs[q].at[b], bufs[q].at[b], sz_sem.at[q, zb], recv_sem.at[q, b], me + (4 if up else -4))

    def send_end(b, up):
        return remote(xbuf.at[b], xbuf.at[b], sx_sem.at[1 - up], recv_sem.at[0, b], me + (4 if up else -4))

    for q in range(2):
        own[q].wait()
        send_y(q, z, me).start()

        @pl.when(z < 3)
        def _():
            send_own(q, 1).start()

        @pl.when(z > 0)
        def _():
            send_own(q, 0).start()
        send_d(q, z, y, me).start()

    def send_table(d):
        dest = lax.rem(me + d, 16)
        return remote(table.at[dest], tbuf.at[me], gs_sem.at[d], gr_sem.at[me], dest)

    @pl.loop(1, 16)
    def _(d):
        send_table(d).start()
    tbuf[me] = table[me]

    def arrive(t):
        zb, yb, col = visit(t)
        b = bid(zb, yb, c)
        middle = zb * (3 - zb)
        for q in range(2):
            send_d(q, zb, yb, b).wait_recv()

            @pl.when(col == 0)
            def _():
                if q:
                    send_y(q, zb, b).start()
                else:
                    @pl.when(middle > 0)
                    def _():
                        send_y(q, zb, b).start()

                @pl.when((zb > z) & (z > 0))
                def _():
                    send_fwd(q, zb, b, 0).start()

                @pl.when((zb < z) & (z < 3))
                def _():
                    send_fwd(q, zb, b, 1).start()
            if q == 0:
                @pl.when((col == 1) & (zb == 3) & (z > 0))
                def _():
                    send_end(b, 0).start()

                @pl.when((col == 1) & (zb == 0) & (z < 3))
                def _():
                    send_end(b, 1).start()
            send_d(q, zb, yb, b).start()

    def flush(t, start):
        zb, yb, _ = visit(t)
        two = pl.ds(bid(zb, yb, 0), 2)
        cps = [pltpu.make_async_copy(xst, x_all.at[:, two], out_sem.at[0, t]),
               pltpu.make_async_copy(zst, z_all.at[:, two], out_sem.at[1, t]),
               pltpu.make_async_copy(hst, hid_all.at[:, two], out_sem.at[2, t]),
               pltpu.make_async_copy(act.at[:, two], act_all.at[:, two], out_sem.at[3, t])]
        if start:
            for cp in cps:
                cp.start()
        else:
            for cp in cps[:3]:
                cp.wait()

    def compute(t):
        zb, yb, _ = visit(t)
        b0 = bid(zb, yb, 0)
        bp = bid(zb, yb, 1 - c)
        for q in range(2):
            send_d(q, zb, yb, bp).wait_recv()
        for p in range(2):
            @pl.when(b0 + p != me)
            def _():
                remote(table.at[0], tbuf.at[b0 + p], gs_sem.at[0], gr_sem.at[b0 + p], partner).wait_recv()

        @pl.when(t > 0)
        def _():
            flush(t - 1, False)
        row = lax.broadcasted_iota(jnp.int32, (2 * cap, tok), 0).astype(F32)
        for p in range(2):
            info = tbuf[b0 + p]
            top = row < cap
            chosen = jnp.where(top, info[2:3, :], info[3:4, :] + cap) == row
            gate = jnp.sum(jnp.where(chosen, jnp.where(top, info[0:1, :], info[1:2, :]), 0.0), axis=1, keepdims=True)
            sel = chosen.astype(BF16)
            pick[b0 + p] = sel
            for n in range(dim // tile):
                cols = slice(n * tile, (n + 1) * tile)
                xr = dot_nn(sel, xbuf[b0 + p, :, cols]).astype(BF16)
                zr = (dot_nn(sel, dybuf[b0 + p, :, cols]) * gate).astype(BF16)
                for e in range(2):
                    xst[e, p, :, cols] = xr[e * cap:(e + 1) * cap]
                    zst[e, p, :, cols] = zr[e * cap:(e + 1) * cap]
        two = pl.ds(b0, 2)
        for e in range(2):
            ab = dot_nn(xst[e].reshape(2 * cap, dim), w13[e]).astype(BF16)
            grad_hidden = dot_nt(zst[e].reshape(2 * cap, dim), w2[e])
            hidden, grad_gate, grad_up = swiglu_parts(ab[:, :ff], ab[:, ff:], grad_hidden)
            hst[e] = hidden.reshape(2, cap, ff)
            act[e, two, :, :ff] = grad_gate.reshape(2, cap, ff)
            act[e, two, :, ff:] = grad_up.reshape(2, cap, ff)
        flush(t, True)

    for cp in shared_load:
        cp.wait()
    ab = dot_nn(xbuf[me], w13[1]).astype(BF16)
    hidden, grad_gate, grad_up = swiglu_parts(ab[:, :ff], ab[:, ff:], dot_nt(dybuf[me], w2[1]))
    shid[...] = hidden
    sact[:, :ff] = grad_gate
    sact[:, ff:] = grad_up
    for n in range(dim // tile):
        cols = slice(n * tile, (n + 1) * tile)
        sdx[:, cols] = dot_nt(sact[...], w13[1, cols, :])
    shared_out = [pltpu.make_async_copy(sact, sact_out, load_sem.at[0]), pltpu.make_async_copy(shid, shid_out, load_sem.at[1])]
    for cp in shared_out + second_load:
        cp.start()
    for cp in first_load + second_load:
        cp.wait()
    compute(0)

    @pl.loop(1, 8)
    def _(t):
        arrive(t)
        compute(t)

    def rs_visit(j):
        late = lax.div(j, 4)
        zb = order(3 - lax.rem(j, 4))
        col = 1 - late
        return zb, y + col * (1 - 2 * y)

    def give(j):
        return remote(dsend.at[lax.rem(j, 2)], pbuf.at[lax.rem(j, 2)], ds_sem.at[lax.rem(j, 2)], dr_sem.at[lax.rem(j, 2)], partner)

    def part(h):
        return pl.ds(h * half, half)

    def rs_y(j, zb, h):
        return remote(sums.at[j, :, part(h)], ybuf.at[zb, :, part(h)], ys_sem.at[zb, h], yr_sem.at[zb, h], side)

    def rs_end(j, end):
        return remote(sums.at[j, :, part(0)], ebuf.at[end], es_sem.at[end], er_sem.at[end], me + 8 * end - 4)

    def rs_compute(j):
        zb, yb = rs_visit(j)
        b = bid(zb, yb, c)
        bp = bid(zb, yb, 1 - c)

        @pl.when(j >= 2)
        def _():
            give(j).wait_send()

        @pl.loop(0, dim // tile)
        def _(n):
            cols = pl.ds(pl.multiple_of(n * tile, tile), tile)
            r = [dot_nt(jnp.concatenate([act[e, b], act[e, bp]], axis=0), w13[e, cols, :]).astype(BF16) for e in range(2)]
            sums[j, :, cols] = dot_tn(pick[b], jnp.concatenate([r[0][:cap], r[1][:cap]], axis=0))
            dsend[lax.rem(j, 2), :, cols] = dot_tn(pick[bp], jnp.concatenate([r[0][cap:], r[1][cap:]], axis=0))

        @pl.when(j >= 2)
        def _():
            pl.semaphore_wait(credit, 1)
        give(j).start()

    def rs_finish(j):
        give(j).wait_recv()
        sums[j] = sums[j] + pbuf[lax.rem(j, 2)]

        @pl.when(j < 6)
        def _():
            pl.semaphore_signal(credit, inc=1, device_id={'ep': partner}, device_id_type=pl.DeviceIdType.MESH)

        @pl.when((j == 0) & (inner == 0))
        def _():
            rs_end(0, far_end).start()

        @pl.when(j < 4)
        def _():
            zb, _ = rs_visit(j)
            rs_y(j, zb, 1).start()

            @pl.when(zb * (3 - zb) > 0)
            def _():
                rs_y(j, zb, 0).start()

    @pl.loop(0, 9)
    def _(j):
        @pl.when(j < 8)
        def _():
            rs_compute(j)

        @pl.when(j > 0)
        def _():
            rs_finish(j - 1)

    def end_in(j, end):
        rs_end(j, end).wait_recv()
        sums[j, :, part(0)] = sums[j, :, part(0)] + ebuf[end]

    def chain(k, h, zb, up):
        j = 7 - k
        slot, gap = (0, zb - z - 1) if up else (1, z - zb - 1)
        return remote(sums.at[j, :, part(h)], cbuf.at[slot, gap, :, part(h)], cs_sem.at[k, h], cr_sem.at[slot, gap, h], me + (4 if up else -4))

    def chain_in(j, h, slot, gap):
        remote(sums.at[j, :, part(h)], cbuf.at[slot, gap, :, part(h)], cs_sem.at[0, h], cr_sem.at[slot, gap, h], partner).wait_recv()
        sums[j, :, part(h)] = sums[j, :, part(h)] + cbuf[slot, gap, :, part(h)]

    def y_in(j, zb, h):
        rs_y(0, zb, h).wait_recv()
        sums[j, :, part(h)] = sums[j, :, part(h)] + ybuf[zb, :, part(h)]

    def step(k, h):
        zb = order(k)
        j = 7 - k
        if h == 1 or k == 2:
            y_in(j, zb, h)
        elif k == 1:
            @pl.when(zb * (3 - zb) > 0)
            def _():
                y_in(j, zb, h)

        @pl.when(zb > z)
        def _():
            @pl.when(z > 0)
            def _():
                chain_in(j, h, 0, zb - z)
            chain(k, h, zb, True).start()

        @pl.when(zb < z)
        def _():
            @pl.when(z < 3)
            def _():
                chain_in(j, h, 1, z - zb)
            chain(k, h, zb, False).start()

    @pl.when(inner > 0)
    def _():
        end_in(0, far_end)
        rs_end(0, far_end).start()
    step(3, 0)

    @pl.when(inner > 0)
    def _():
        end_in(2, near_end)
        rs_end(2, near_end).start()
    step(3, 1)
    step(2, 0)

    @pl.when(inner == 0)
    def _():
        end_in(3, near_end)
        rs_y(3, z, 0).start()
    step(2, 1)
    step(1, 0)
    step(1, 1)
    flush(7, False)
    for h in range(2):
        @pl.when(z > 0)
        def _():
            chain_in(7, h, 0, 0)

        @pl.when(z < 3)
        def _():
            chain_in(7, h, 1, 0)
        rs_y(0, z, h).wait_recv()
        total = sums[7, :, part(h)] + ybuf[z, :, part(h)] + sdx[:, part(h)]
        xst[0, :, :, part(h)] = total.astype(BF16).reshape(2, cap, half)
    result = pltpu.make_async_copy(xst.at[0], grad_x, load_sem.at[2])
    result.start()

    for cp in shared_out:
        cp.wait()
    for t in range(8):
        pltpu.make_async_copy(act.at[:, pl.ds(0, 2)], act_all.at[:, pl.ds(0, 2)], out_sem.at[3, t]).wait()
    for zb in range(4):
        for q in range(2):
            if q or zb in (1, 2):
                send_y(q, zb, 0).wait_send()
            else:
                @pl.when(z == zb)
                def _():
                    send_y(q, zb, 0).wait_send()
            for yb in range(2):
                send_d(q, zb, yb, 0).wait_send()

            @pl.when(((zb > z) & (z > 0)) | ((zb < z) & (z < 3)))
            def _():
                send_fwd(q, zb, 0, 1).wait_send()
        for h in range(2):
            if h or zb in (1, 2):
                rs_y(0, zb, h).wait_send()
            else:
                @pl.when(z == zb)
                def _():
                    rs_y(0, zb, h).wait_send()
            if zb:
                remote(sums.at[0, :, part(h)], cbuf.at[0, 0, :, part(h)], cs_sem.at[zb, h], cr_sem.at[0, 0, h], partner).wait_send()

    @pl.when(z < 3)
    def _():
        send_end(0, 1).wait_send()
        for q in range(2):
            send_own(q, 1).wait_send()

    @pl.when(z > 0)
    def _():
        send_end(0, 0).wait_send()
        for q in range(2):
            send_own(q, 0).wait_send()
    rs_end(0, far_end).wait_send()

    @pl.when(inner > 0)
    def _():
        rs_end(0, near_end).wait_send()

    @pl.loop(1, 16)
    def _(d):
        send_table(d).wait_send()
    for j in range(2):
        give(j).wait_send()
    result.wait()


def routed(x_tokens, dy_tokens, table, w_gate, w_up, w_down, s_gate, s_up, s_down):
    tok, dim = x_tokens.shape
    ff = w_gate.shape[2]
    cap = tok // 2
    dma = pltpu.SemaphoreType.DMA
    shape = jax.ShapeDtypeStruct
    return pl.pallas_call(
        routed_kernel,
        name='routed',
        out_shape=(shape((2, cap, dim), BF16), shape((2, 16, cap, dim), BF16), shape((2, 16, cap, dim), BF16),
                   shape((2, 16, cap, 2 * ff), BF16), shape((2, 16, cap, ff), BF16), shape((tok, 2 * ff), BF16), shape((tok, ff), BF16)),
        in_specs=[ANY, ANY, VMEM] + [ANY] * 6,
        out_specs=(ANY,) * 7,
        scratch_shapes=[
            pltpu.VMEM((16, tok, dim), BF16), pltpu.VMEM((16, tok, dim), BF16), pltpu.VMEM((16, 8, tok), F32), pltpu.VMEM((16, 2 * cap, tok), BF16),
            pltpu.VMEM((2, dim, 2 * ff), BF16), pltpu.VMEM((2, ff, dim), BF16),
            pltpu.VMEM((2, 16, cap, 2 * ff), BF16), pltpu.VMEM((2, 2, cap, ff), BF16), pltpu.VMEM((2, 2, cap, dim), BF16), pltpu.VMEM((2, 2, cap, dim), BF16),
            pltpu.VMEM((tok, 2 * ff), BF16), pltpu.VMEM((tok, ff), BF16), pltpu.VMEM((tok, dim), F32),
            pltpu.VMEM((8, tok, dim), F32), pltpu.VMEM((2, tok, dim), F32), pltpu.VMEM((2, tok, dim), F32),
            pltpu.VMEM((4, tok, dim), F32), pltpu.VMEM((2, 3, tok, dim), F32), pltpu.VMEM((2, tok, dim // 2), F32),
            dma((8,)), dma((4, 8)), dma((16,)), dma((16,)), dma((2, 16)), dma((2, 4)), dma((2, 8)), dma((2, 2)), dma((2, 4)), dma((2,)),
            dma((2,)), dma((2,)), dma((4, 2)), dma((4, 2)), dma((4, 2)), dma((2, 3, 2)), dma((2,)), dma((2,)), pltpu.SemaphoreType.REGULAR,
        ],
        compiler_params=pltpu.CompilerParams(collective_id=0, has_side_effects=True, vmem_limit_bytes=VMEM_LIMIT),
        cost_estimate=pl.CostEstimate(flops=16 * tok * 2 * dim * ff * 5, bytes_accessed=80_000_000, transcendentals=0),
    )(x_tokens, dy_tokens, table, w_gate, w_up, w_down, s_gate, s_up, s_down)


def up_grad_kernel(x, act, g1, g3):
    ff = g1.shape[2]
    both = dot_tn(x[0], act[0])
    g1[0] = both[:, :ff]
    g3[0] = both[:, ff:]


def up_grads(x, act):
    experts, rows, dim = x.shape
    ff = act.shape[2] // 2
    tile = min(512, dim)
    out = jax.ShapeDtypeStruct((experts, dim, ff), F32)
    return pl.pallas_call(
        up_grad_kernel,
        name='up_grads',
        out_shape=(out, out),
        grid=(experts, dim // tile),
        in_specs=[pl.BlockSpec((1, rows, tile), lambda e, i: (e, 0, i)), pl.BlockSpec((1, rows, 2 * ff), lambda e, i: (e, 0, 0))],
        out_specs=(pl.BlockSpec((1, tile, ff), lambda e, i: (e, i, 0)),) * 2,
        compiler_params=pltpu.CompilerParams(vmem_limit_bytes=60_000_000),
        cost_estimate=pl.CostEstimate(flops=4 * experts * rows * dim * ff, bytes_accessed=8 * experts * dim * ff + 2 * x.size + 2 * act.size, transcendentals=0),
    )(x, act)


def down_grad_kernel(hid, dz, g2):
    g2[0] = dot_tn(hid[0], dz[0])


def down_grads(hid, dz):
    experts, rows, dim = dz.shape
    ff = hid.shape[2]
    tile = min(512, dim)
    return pl.pallas_call(
        down_grad_kernel,
        name='down_grads',
        out_shape=jax.ShapeDtypeStruct((experts, ff, dim), F32),
        grid=(experts, dim // tile),
        in_specs=[pl.BlockSpec((1, rows, ff), lambda e, n: (e, 0, 0)), pl.BlockSpec((1, rows, tile), lambda e, n: (e, 0, n))],
        out_specs=pl.BlockSpec((1, ff, tile), lambda e, n: (e, 0, n)),
        compiler_params=pltpu.CompilerParams(vmem_limit_bytes=60_000_000),
        cost_estimate=pl.CostEstimate(flops=2 * experts * rows * dim * ff, bytes_accessed=4 * experts * dim * ff + 2 * hid.size + 2 * dz.size, transcendentals=0),
    )(hid, dz)


def shared_grad_kernel(x, dy, act, hid, g1, g3, g2):
    ff = hid.shape[1]
    both = dot_tn(x[...], act[...])
    g1[0] = both[:, :ff]
    g3[0] = both[:, ff:]
    g2[0] = dot_tn(hid[...], dy[...])


def shared_grads(x, dy, act, hid):
    tok, dim = x.shape
    ff = hid.shape[1]
    tile = min(512, dim)
    out = jax.ShapeDtypeStruct((1, dim, ff), F32)
    return pl.pallas_call(
        shared_grad_kernel,
        name='shared_grads',
        out_shape=(out, out, jax.ShapeDtypeStruct((1, ff, dim), F32)),
        grid=(dim // tile,),
        in_specs=[pl.BlockSpec((tok, tile), lambda i: (0, i)), pl.BlockSpec((tok, tile), lambda i: (0, i)), pl.BlockSpec((tok, 2 * ff), lambda i: (0, 0)), pl.BlockSpec((tok, ff), lambda i: (0, 0))],
        out_specs=(pl.BlockSpec((1, tile, ff), lambda i: (0, i, 0)),) * 2 + (pl.BlockSpec((1, ff, tile), lambda i: (0, 0, i)),),
        compiler_params=pltpu.CompilerParams(vmem_limit_bytes=60_000_000),
        cost_estimate=pl.CostEstimate(flops=6 * tok * dim * ff, bytes_accessed=12 * dim * ff + 4 * x.size, transcendentals=0),
    )(x, dy, act, hid)


def solution(mesh):
    group = mesh.shape['ep']
    token_spec = P(('dp', 'ep'), None)
    expert_spec = P('ep', None, None)
    whole_spec = P(None, None)
    grad_spec = P(('dp', 'ep'), None, None)

    def local_backward(x_tokens, dy_tokens, expert_ids, gate_vals, slot_pos, w_gate, w_up, w_down, shared_gate, shared_up, shared_down):
        tok, dim = x_tokens.shape
        local_experts = w_gate.shape[0]
        experts = jnp.arange(group * local_experts, dtype=jnp.int32)
        hit = (expert_ids.T[None] == experts[:, None, None]) & (slot_pos.T[None] >= 0)
        gates = jnp.sum(jnp.where(hit, gate_vals.T[None], 0.0), axis=1)
        slots = jnp.sum(jnp.where(hit, slot_pos.T[None].astype(F32) + 1.0, 0.0), axis=1) - 1.0
        table = jnp.concatenate([gates.reshape(group, local_experts, tok), slots.reshape(group, local_experts, tok), jnp.zeros((group, 8 - 2 * local_experts, tok), F32)], axis=1)
        grad_x, x_all, z_all, act_all, hid_all, sact, shid = routed(x_tokens, dy_tokens, table, w_gate, w_up, w_down, shared_gate, shared_up, shared_down)
        x_all, z_all, act_all, hid_all = [a.reshape(local_experts, -1, a.shape[-1]) for a in (x_all, z_all, act_all, hid_all)]
        grad_w_gate, grad_w_up = up_grads(x_all, act_all)
        grad_w_down = down_grads(hid_all, z_all)
        grad_shared_gate, grad_shared_up, grad_shared_down = shared_grads(x_tokens, dy_tokens, sact, shid)
        grad_x = grad_x.reshape(tok, dim)
        return grad_x, grad_w_gate, grad_w_up, grad_w_down, grad_shared_gate, grad_shared_up, grad_shared_down

    return jax.shard_map(local_backward, mesh=mesh, in_specs=(token_spec, token_spec, token_spec, token_spec, token_spec, expert_spec, expert_spec, expert_spec, whole_spec, whole_spec, whole_spec), out_specs=(token_spec, grad_spec, grad_spec, grad_spec, grad_spec, grad_spec, grad_spec), check_vma=False)
```

time: 271 us -> 252 us (0.930)
  Pallas kernels: 266 us -> 247 us
    pallas_call x1, Pallas kernels: 27.6 us -> 15.7 us  [up_grads(): pl.pallas_call(up_grad_kernel, name='up_grads', out_shape=(out, out), gri...]
    pallas_call x1, Pallas kernels: 16.7 us -> 11.9 us  [down_grads(): pl.pallas_call(down_grad_kernel, name='down_grads', out_shape=jax.ShapeDt...]
where the time goes in v3:
time: 252 us
  Pallas kernels  247 us (98%)
  other arithmetic  2.87 us (1%)
    pallas_call x1, Pallas kernels, routed(): pl.pallas_call(routed_kernel, name='routed', out_shape=(shape((2, cap, di...  213 us
    pallas_call x1, Pallas kernels, up_grads(): pl.pallas_call(up_grad_kernel, name='up_grads', out_shape=(out, out), gri...  15.7 us
    pallas_call x1, Pallas kernels, down_grads(): pl.pallas_call(down_grad_kernel, name='down_grads', out_shape=jax.ShapeDt...  11.9 us
    pallas_call x1, Pallas kernels, shared_grads(): pl.pallas_call(shared_grad_kernel, name='shared_grads', out_shape=(out, o...  6.29 us

profile of v3, /device:TPU:0, one launch (start us, length us, event | category | flops | bytes accessed | tf_op | source)
XLA Modules:
  0.0 251.8 jit_solution(6120236213501380008)
XLA Ops:
  0.6 0.1 pad.2.clone
  0.7 0.7 compare_bitcast_fusion
  1.4 0.7 add_bitcast_fusion
  2.1 0.8 select_reduce_fusion.1
  2.9 0.7 maximum_maximum_fusion.table
  3.6 213.5 %routed.1 = (bf16[2,64,2048]{2,1,0:T(8,128)(2,1)}, bf16[2,16,64,2048]{3,2,1,0:T(8,128)(2,1)}, bf16[2,16,64,2048]{3,2,1,0:T(8,128)(2,1)}, bf16[2,16,64,1024]{3,2,...) custom-call(bf16[128,2048]{1,0:T(8,128)(2,1)} %x.1, ...), custom_call_target="tpu_custom_call" | custom-call | flops 21474836480 | bytes 80000000 | tf_op jit(solution)/shard_map/routed/pallas_call | solution.py:451
  217.1 15.7 %up_grads.1 = (f32[2,2048,512]{2,1,0:T(8,128)}, f32[2,2048,512]{2,1,0:T(8,128)}) custom-call(bf16[2,1024,2048]{2,1,0:T(8,128)(2,1)} %bitcast.20, bf16[2,1024,1024]{2,1,0:T(8,128)(2,1)} %bitcast.21), custom_call_target="tpu_custom_call" | custom-call | flops 8589934592 | bytes 29360128 | tf_op jit(solution)/shard_map/up_grads/pallas_call | solution.py:485
  232.8 0.0 copy-start
  232.8 11.9 %down_grads.1 = f32[2,512,2048]{2,1,0:T(8,128)} custom-call(bf16[2,1024,512]{2,1,0:T(8,128)(2,1)} %bitcast.14, bf16[2,1024,2048]{2,1,0:T(8,128)(2,1)} %bitcast.13), custom_call_target="tpu_custom_call" | custom-call | flops 4294967296 | bytes 18874368 | tf_op jit(solution)/shard_map/down_grads/pallas_call | solution.py:505
  244.7 6.3 %shared_grads.1 = (f32[1,2048,512]{2,1,0:T(8,128)}, f32[1,2048,512]{2,1,0:T(8,128)}, f32[1,512,2048]{2,1,0:T(8,128)}) custom-call(bf16[128,2048]{1,0:T(8,128)(2,1)} %x.1, bf16[128,2048]{1,0:T(8,128)(2,1)} %dy.1, bf16[128,1024]{1,0:T(8,128)(2,1)} %get-tuple-element.26.act, bf16[128,512]{1,0:T(8,128)(2,1)} %get-tuple-element.27.hid), custom_call_target="tpu_custom_call" | custom-call | flops 805306368 | bytes 13631488 | tf_op jit(solution)/shard_map/shared_grads/pallas_call | solution.py:530
  251.0 0.0 copy-done
  251.0 0.8 copy.19
  (2 shorter events, 0.0 us)
Async XLA Ops:
  232.8 18.2 %copy-start = (bf16[2,64,2048]{2,1,0:T(8,128)(2,1)S(1)}, bf16[2,64,2048]{2,1,0:T(8,128)(2,1)}, u32[]{:S(2)}) copy-start(bf16[2,64,2048]{2,1,0:T(8,128)(2,1)} %get-tuple-element.19) | copy-start | bytes 1572868

commit v4 on v3

--- a/solution.py
+++ b/solution.py
@@ -236,19 +236,6 @@
         cp.start()
     for cp in first_load + second_load:
         cp.wait()
-    compute(0)
-
-    @pl.loop(1, 8)
-    def _(t):
-        arrive(t)
-        compute(t)
-
-    def rs_visit(j):
-        late = lax.div(j, 4)
-        zb = order(3 - lax.rem(j, 4))
-        col = 1 - late
-        return zb, y + col * (1 - 2 * y)
-
     def give(j):
         return remote(dsend.at[lax.rem(j, 2)], pbuf.at[lax.rem(j, 2)], ds_sem.at[lax.rem(j, 2)], dr_sem.at[lax.rem(j, 2)], partner)
 
@@ -262,7 +249,7 @@
         return remote(sums.at[j, :, part(0)], ebuf.at[end], es_sem.at[end], er_sem.at[end], me + 8 * end - 4)
 
     def rs_compute(j):
-        zb, yb = rs_visit(j)
+        zb, yb, _ = visit(j)
         b = bid(zb, yb, c)
         bp = bid(zb, yb, 1 - c)
 
@@ -290,35 +277,15 @@
         def _():
             pl.semaphore_signal(credit, inc=1, device_id={'ep': partner}, device_id_type=pl.DeviceIdType.MESH)
 
-        @pl.when((j == 0) & (inner == 0))
-        def _():
-            rs_end(0, far_end).start()
-
-        @pl.when(j < 4)
-        def _():
-            zb, _ = rs_visit(j)
-            rs_y(j, zb, 1).start()
-
-            @pl.when(zb * (3 - zb) > 0)
-            def _():
-                rs_y(j, zb, 0).start()
-
-    @pl.loop(0, 9)
-    def _(j):
-        @pl.when(j < 8)
-        def _():
-            rs_compute(j)
-
-        @pl.when(j > 0)
-        def _():
-            rs_finish(j - 1)
+    own_slot = (0, 1, 3, 5)
+    other_slot = (2, 4, 6, 7)
 
     def end_in(j, end):
         rs_end(j, end).wait_recv()
         sums[j, :, part(0)] = sums[j, :, part(0)] + ebuf[end]
 
     def chain(k, h, zb, up):
-        j = 7 - k
+        j = own_slot[k]
         slot, gap = (0, zb - z - 1) if up else (1, z - zb - 1)
         return remote(sums.at[j, :, part(h)], cbuf.at[slot, gap, :, part(h)], cs_sem.at[k, h], cr_sem.at[slot, gap, h], me + (4 if up else -4))
 
@@ -332,7 +299,7 @@
 
     def step(k, h):
         zb = order(k)
-        j = 7 - k
+        j = own_slot[k]
         if h == 1 or k == 2:
             y_in(j, zb, h)
         elif k == 1:
@@ -354,37 +321,77 @@
                 chain_in(j, h, 1, z - zb)
             chain(k, h, zb, False).start()
 
+    def scatter_y(k):
+        zb = order(k)
+        rs_y(other_slot[k], zb, 1).start()
+        if k == 2:
+            rs_y(other_slot[k], zb, 0).start()
+        elif k == 1:
+            @pl.when(zb * (3 - zb) > 0)
+            def _():
+                rs_y(other_slot[k], zb, 0).start()
+        elif k == 0:
+            @pl.when(inner > 0)
+            def _():
+                rs_y(other_slot[k], zb, 0).start()
+
+    @pl.loop(0, 8)
+    def _(t):
+        @pl.when(t > 0)
+        def _():
+            arrive(t)
+        compute(t)
+        rs_compute(t)
+        rs_finish(t)
+
+        @pl.when((t == 5) & (inner == 0))
+        def _():
+            step(3, 0)
+
+        @pl.when(t == 6)
+        def _():
+            scatter_y(2)
+
+    scatter_y(3)
+
+    @pl.when(inner == 0)
+    def _():
+        rs_end(other_slot[3], far_end).start()
+    scatter_y(1)
+    scatter_y(0)
+
     @pl.when(inner > 0)
     def _():
-        end_in(0, far_end)
-        rs_end(0, far_end).start()
-    step(3, 0)
-
-    @pl.when(inner > 0)
-    def _():
-        end_in(2, near_end)
-        rs_end(2, near_end).start()
+        step(3, 0)
+        step(1, 0)
+        end_in(other_slot[3], far_end)
+        rs_end(other_slot[3], far_end).start()
+        end_in(other_slot[1], near_end)
+        rs_end(other_slot[1], near_end).start()
+    step(2, 1)
+    step(2, 0)
     step(3, 1)
-    step(2, 0)
 
     @pl.when(inner == 0)
     def _():
-        end_in(3, near_end)
-        rs_y(3, z, 0).start()
-    step(2, 1)
-    step(1, 0)
+        end_in(other_slot[0], near_end)
+        rs_y(other_slot[0], z, 0).start()
     step(1, 1)
+
+    @pl.when(inner == 0)
+    def _():
+        step(1, 0)
     flush(7, False)
     for h in range(2):
         @pl.when(z > 0)
         def _():
-            chain_in(7, h, 0, 0)
+            chain_in(0, h, 0, 0)
 
         @pl.when(z < 3)
         def _():
-            chain_in(7, h, 1, 0)
+            chain_in(0, h, 1, 0)
         rs_y(0, z, h).wait_recv()
-        total = sums[7, :, part(h)] + ybuf[z, :, part(h)] + sdx[:, part(h)]
+        total = sums[0, :, part(h)] + ybuf[z, :, part(h)] + sdx[:, part(h)]
         xst[0, :, :, part(h)] = total.astype(BF16).reshape(2, cap, half)
     result = pltpu.make_async_copy(xst.at[0], grad_x, load_sem.at[2])
     result.start()

time: 252 us -> 249 us (0.988)
  Pallas kernels: 247 us -> 244 us
    pallas_call x1, Pallas kernels: 213 us -> 210 us  [routed(): pl.pallas_call(routed_kernel, name='routed', out_shape=(shape((2, cap, di...]
where the time goes in v4:
time: 249 us; the launch traced here: 248 us
  Pallas kernels  244 us (98%)
  other arithmetic  2.87 us (1%)
    pallas_call x1, Pallas kernels, routed(): pl.pallas_call(routed_kernel, name='routed', out_shape=(shape((2, cap, di...  210 us
    pallas_call x1, Pallas kernels, up_grads(): pl.pallas_call(up_grad_kernel, name='up_grads', out_shape=(out, out), gri...  15.7 us
    pallas_call x1, Pallas kernels, down_grads(): pl.pallas_call(down_grad_kernel, name='down_grads', out_shape=jax.ShapeDt...  11.9 us
    pallas_call x1, Pallas kernels, shared_grads(): pl.pallas_call(shared_grad_kernel, name='shared_grads', out_shape=(out, o...  6.29 us

profile of v4, /device:TPU:0, one launch (start us, length us, event | category | flops | bytes accessed | tf_op | source)
XLA Modules:
  0.0 248.3 jit_solution(17635540661587164837)
XLA Ops:
  0.6 0.1 pad.2.clone
  0.7 0.7 compare_bitcast_fusion
  1.4 0.7 add_bitcast_fusion
  2.1 0.8 select_reduce_fusion.1
  2.9 0.7 maximum_maximum_fusion.table
  3.6 210.0 %routed.1 = (bf16[2,64,2048]{2,1,0:T(8,128)(2,1)}, bf16[2,16,64,2048]{3,2,1,0:T(8,128)(2,1)}, bf16[2,16,64,2048]{3,2,1,0:T(8,128)(2,1)}, bf16[2,16,64,1024]{3,2,...) custom-call(bf16[128,2048]{1,0:T(8,128)(2,1)} %x.1, ...), custom_call_target="tpu_custom_call" | custom-call | flops 21474836480 | bytes 80000000 | tf_op jit(solution)/shard_map/routed/pallas_call | solution.py:458
  213.6 15.7 %up_grads.1 = (f32[2,2048,512]{2,1,0:T(8,128)}, f32[2,2048,512]{2,1,0:T(8,128)}) custom-call(bf16[2,1024,2048]{2,1,0:T(8,128)(2,1)} %bitcast.20, bf16[2,1024,1024]{2,1,0:T(8,128)(2,1)} %bitcast.21), custom_call_target="tpu_custom_call" | custom-call | flops 8589934592 | bytes 29360128 | tf_op jit(solution)/shard_map/up_grads/pallas_call | solution.py:492
  229.3 0.0 copy-start
  229.3 11.9 %down_grads.1 = f32[2,512,2048]{2,1,0:T(8,128)} custom-call(bf16[2,1024,512]{2,1,0:T(8,128)(2,1)} %bitcast.14, bf16[2,1024,2048]{2,1,0:T(8,128)(2,1)} %bitcast.13), custom_call_target="tpu_custom_call" | custom-call | flops 4294967296 | bytes 18874368 | tf_op jit(solution)/shard_map/down_grads/pallas_call | solution.py:512
  241.2 6.3 %shared_grads.1 = (f32[1,2048,512]{2,1,0:T(8,128)}, f32[1,2048,512]{2,1,0:T(8,128)}, f32[1,512,2048]{2,1,0:T(8,128)}) custom-call(bf16[128,2048]{1,0:T(8,128)(2,1)} %x.1, bf16[128,2048]{1,0:T(8,128)(2,1)} %dy.1, bf16[128,1024]{1,0:T(8,128)(2,1)} %get-tuple-element.26.act, bf16[128,512]{1,0:T(8,128)(2,1)} %get-tuple-element.27.hid), custom_call_target="tpu_custom_call" | custom-call | flops 805306368 | bytes 13631488 | tf_op jit(solution)/shard_map/shared_grads/pallas_call | solution.py:537
  247.5 0.0 copy-done
  247.5 0.8 copy.19
  (2 shorter events, 0.0 us)
Async XLA Ops:
  229.3 18.2 %copy-start = (bf16[2,64,2048]{2,1,0:T(8,128)(2,1)S(1)}, bf16[2,64,2048]{2,1,0:T(8,128)(2,1)}, u32[]{:S(2)}) copy-start(bf16[2,64,2048]{2,1,0:T(8,128)(2,1)} %get-tuple-element.19) | copy-start | bytes 1572868

commit v5 on v4

--- a/solution.py
+++ b/solution.py
@@ -35,6 +35,29 @@
     grad_gate = (grad_hidden * up_f32 * sigma * (1.0 + gate_f32 * (1.0 - sigma))).astype(BF16)
     grad_up = (grad_hidden * silu_gate).astype(BF16)
     return hidden, grad_gate, grad_up
+
+
+END_PLAN = (
+    'F10F11F20C00F40R00C10F30R10F41X00F21X10C20R20F31C30R30F50X20',
+    'X30C40F51F60R40C50X40Y11F61R50C60R60X50S30F70F71X60C70R70Y21',
+    'X70Y31E00Y20Y10S21S31Y01S20S11S10N00',
+)
+MID_PLAN = (
+    'C00F10F30F20R00F31F11C10F50X00F60R10F21C20R20X10F51C30F61F40',
+    'X20F41R30C40R40F70C50X30X40R50F71C60R60Y01X50C70S30Y11X60R70',
+    'X70Y21E00S10Y31N00Y20S21S31Y00S20S11',
+)
+
+
+def gaps(text):
+    found = [[]]
+    for i in range(0, len(text), 3):
+        token = text[i:i + 3]
+        if token[0] in 'CR':
+            found.append([])
+        else:
+            found[-1].append(token)
+    return found
 
 
 def routed_kernel(x_in, dy_in, table, w_gate, w_up, w_down, s_gate, s_up, s_down,
@@ -58,6 +81,9 @@
     near_end = lax.div(z, 2)
     far_end = 1 - near_end
     bufs = (xbuf, dybuf)
+    own_slot = (0, 1, 3, 5)
+    other_slot = (2, 4, 6, 7)
+    near_first = [(own_slot.index(t), 0) if t in own_slot else (other_slot.index(t), 1) for t in range(8)]
 
     def bid(zz, yy, cc):
         return zz * 4 + yy * 2 + cc
@@ -135,38 +161,38 @@
         send_table(d).start()
     tbuf[me] = table[me]
 
-    def arrive(t):
-        zb, yb, col = visit(t)
+    def place(t):
+        k, col = near_first[t]
+        return order(k), y + col * (1 - 2 * y), col
+
+    def pass_on(t, q):
+        zb, yb, col = place(t)
         b = bid(zb, yb, c)
-        middle = zb * (3 - zb)
-        for q in range(2):
-            send_d(q, zb, yb, b).wait_recv()
-
-            @pl.when(col == 0)
+        send_d(q, zb, yb, b).wait_recv()
+        if col == 0:
+            if q:
+                send_y(q, zb, b).start()
+            else:
+                @pl.when(zb * (3 - zb) > 0)
+                def _():
+                    send_y(q, zb, b).start()
+
+            @pl.when((zb > z) & (z > 0))
             def _():
-                if q:
-                    send_y(q, zb, b).start()
-                else:
-                    @pl.when(middle > 0)
-                    def _():
-                        send_y(q, zb, b).start()
-
-                @pl.when((zb > z) & (z > 0))
-                def _():
-                    send_fwd(q, zb, b, 0).start()
-
-                @pl.when((zb < z) & (z < 3))
-                def _():
-                    send_fwd(q, zb, b, 1).start()
-            if q == 0:
-                @pl.when((col == 1) & (zb == 3) & (z > 0))
-                def _():
-                    send_end(b, 0).start()
-
-                @pl.when((col == 1) & (zb == 0) & (z < 3))
-                def _():
-                    send_end(b, 1).start()
-            send_d(q, zb, yb, b).start()
+                send_fwd(q, zb, b, 0).start()
+
+            @pl.when((zb < z) & (z < 3))
+            def _():
+                send_fwd(q, zb, b, 1).start()
+        elif q == 0:
+            @pl.when((zb == 3) & (z > 0))
+            def _():
+                send_end(b, 0).start()
+
+            @pl.when((zb == 0) & (z < 3))
+            def _():
+                send_end(b, 1).start()
+        send_d(q, zb, yb, b).start()
 
     def flush(t, start):
         zb, yb, _ = visit(t)
@@ -271,14 +297,9 @@
 
     def rs_finish(j):
         give(j).wait_recv()
-        sums[j] = sums[j] + pbuf[lax.rem(j, 2)]
-
-        @pl.when(j < 6)
-        def _():
+        sums[j] = sums[j] + pbuf[j % 2]
+        if j < 6:
             pl.semaphore_signal(credit, inc=1, device_id={'ep': partner}, device_id_type=pl.DeviceIdType.MESH)
-
-    own_slot = (0, 1, 3, 5)
-    other_slot = (2, 4, 6, 7)
 
     def end_in(j, end):
         rs_end(j, end).wait_recv()
@@ -297,92 +318,68 @@
         rs_y(0, zb, h).wait_recv()
         sums[j, :, part(h)] = sums[j, :, part(h)] + ybuf[zb, :, part(h)]
 
-    def step(k, h):
+    def step(k, h, mid):
         zb = order(k)
         j = own_slot[k]
-        if h == 1 or k == 2:
+        if h or k == 2 or (k == 1 and not mid):
             y_in(j, zb, h)
-        elif k == 1:
-            @pl.when(zb * (3 - zb) > 0)
-            def _():
-                y_in(j, zb, h)
 
         @pl.when(zb > z)
         def _():
-            @pl.when(z > 0)
-            def _():
+            if mid:
                 chain_in(j, h, 0, zb - z)
             chain(k, h, zb, True).start()
 
         @pl.when(zb < z)
         def _():
-            @pl.when(z < 3)
-            def _():
+            if mid:
                 chain_in(j, h, 1, z - zb)
             chain(k, h, zb, False).start()
 
-    def scatter_y(k):
-        zb = order(k)
-        rs_y(other_slot[k], zb, 1).start()
-        if k == 2:
-            rs_y(other_slot[k], zb, 0).start()
-        elif k == 1:
-            @pl.when(zb * (3 - zb) > 0)
-            def _():
-                rs_y(other_slot[k], zb, 0).start()
-        elif k == 0:
-            @pl.when(inner > 0)
-            def _():
-                rs_y(other_slot[k], zb, 0).start()
+    def act_on(token, mid):
+        kind, k, h = token[0], int(token[1]), int(token[2])
+        if kind == 'F':
+            pass_on(k, h)
+        elif kind == 'X':
+            rs_finish(k)
+        elif kind == 'Y':
+            rs_y(other_slot[k], order(k), h).start()
+        elif kind == 'S':
+            step(k, h, mid)
+        elif kind == 'E':
+            if mid:
+                end_in(other_slot[3], far_end)
+            rs_end(other_slot[3], far_end).start()
+        elif mid:
+            end_in(other_slot[1], near_end)
+            rs_end(other_slot[1], near_end).start()
+        else:
+            end_in(other_slot[0], near_end)
+            rs_y(other_slot[0], z, 0).start()
+
+    plans = [gaps(''.join(rows)) for rows in (END_PLAN, MID_PLAN)]
+
+    def between(t, gap):
+        for mid in range(2):
+            tokens = plans[mid][gap]
+            if tokens:
+                @pl.when((t == gap // 2) & ((inner > 0) if mid else (inner == 0)))
+                def _():
+                    for token in tokens:
+                        act_on(token, mid)
 
     @pl.loop(0, 8)
     def _(t):
-        @pl.when(t > 0)
-        def _():
-            arrive(t)
+        for g in range(8):
+            between(t, 2 * g)
         compute(t)
+        for g in range(8):
+            between(t, 2 * g + 1)
         rs_compute(t)
-        rs_finish(t)
-
-        @pl.when((t == 5) & (inner == 0))
-        def _():
-            step(3, 0)
-
-        @pl.when(t == 6)
-        def _():
-            scatter_y(2)
-
-    scatter_y(3)
-
-    @pl.when(inner == 0)
-    def _():
-        rs_end(other_slot[3], far_end).start()
-    scatter_y(1)
-    scatter_y(0)
-
-    @pl.when(inner > 0)
-    def _():
-        step(3, 0)
-        step(1, 0)
-        end_in(other_slot[3], far_end)
-        rs_end(other_slot[3], far_end).start()
-        end_in(other_slot[1], near_end)
-        rs_end(other_slot[1], near_end).start()
-    step(2, 1)
-    step(2, 0)
-    step(3, 1)
-
-    @pl.when(inner == 0)
-    def _():
-        end_in(other_slot[0], near_end)
-        rs_y(other_slot[0], z, 0).start()
-    step(1, 1)
-
-    @pl.when(inner == 0)
-    def _():
-        step(1, 0)
+
+    between(8, 16)
     flush(7, False)
-    for h in range(2):
+    for h in (1, 0):
         @pl.when(z > 0)
         def _():
             chain_in(0, h, 0, 0)

time: 249 us -> 225 us (0.904)
  Pallas kernels: 244 us -> 220 us
    pallas_call x1, Pallas kernels: 210 us -> 186 us  [routed(): pl.pallas_call(routed_kernel, name='routed', out_shape=(shape((2, cap, di...]
where the time goes in v5:
time: 225 us; the launch traced here: 224 us
  Pallas kernels  220 us (98%)
  other arithmetic  2.87 us (1%)
    pallas_call x1, Pallas kernels, routed(): pl.pallas_call(routed_kernel, name='routed', out_shape=(shape((2, cap, di...  186 us
    pallas_call x1, Pallas kernels, up_grads(): pl.pallas_call(up_grad_kernel, name='up_grads', out_shape=(out, out), gri...  15.7 us
    pallas_call x1, Pallas kernels, down_grads(): pl.pallas_call(down_grad_kernel, name='down_grads', out_shape=jax.ShapeDt...  11.9 us
    pallas_call x1, Pallas kernels, shared_grads(): pl.pallas_call(shared_grad_kernel, name='shared_grads', out_shape=(out, o...  6.29 us

profile of v5, /device:TPU:0, one launch (start us, length us, event | category | flops | bytes accessed | tf_op | source)
XLA Modules:
  0.0 224.1 jit_solution(11576941358638260028)
XLA Ops:
  0.6 0.1 pad.2.clone
  0.7 0.7 compare_bitcast_fusion
  1.4 0.7 add_bitcast_fusion
  2.1 0.8 select_reduce_fusion.1
  2.9 0.7 maximum_maximum_fusion.table
  3.6 185.7 %routed.1 = (bf16[2,64,2048]{2,1,0:T(8,128)(2,1)}, bf16[2,16,64,2048]{3,2,1,0:T(8,128)(2,1)}, bf16[2,16,64,2048]{3,2,1,0:T(8,128)(2,1)}, bf16[2,16,64,1024]{3,2,...) custom-call(bf16[128,2048]{1,0:T(8,128)(2,1)} %x.1, ...), custom_call_target="tpu_custom_call" | custom-call | flops 21474836480 | bytes 80000000 | tf_op jit(solution)/shard_map/routed/pallas_call | solution.py:455
  189.3 15.7 %up_grads.1 = (f32[2,2048,512]{2,1,0:T(8,128)}, f32[2,2048,512]{2,1,0:T(8,128)}) custom-call(bf16[2,1024,2048]{2,1,0:T(8,128)(2,1)} %bitcast.20, bf16[2,1024,1024]{2,1,0:T(8,128)(2,1)} %bitcast.21), custom_call_target="tpu_custom_call" | custom-call | flops 8589934592 | bytes 29360128 | tf_op jit(solution)/shard_map/up_grads/pallas_call | solution.py:489
  205.1 0.0 copy-start
  205.1 11.9 %down_grads.1 = f32[2,512,2048]{2,1,0:T(8,128)} custom-call(bf16[2,1024,512]{2,1,0:T(8,128)(2,1)} %bitcast.14, bf16[2,1024,2048]{2,1,0:T(8,128)(2,1)} %bitcast.13), custom_call_target="tpu_custom_call" | custom-call | flops 4294967296 | bytes 18874368 | tf_op jit(solution)/shard_map/down_grads/pallas_call | solution.py:509
  217.0 6.3 %shared_grads.1 = (f32[1,2048,512]{2,1,0:T(8,128)}, f32[1,2048,512]{2,1,0:T(8,128)}, f32[1,512,2048]{2,1,0:T(8,128)}) custom-call(bf16[128,2048]{1,0:T(8,128)(2,1)} %x.1, bf16[128,2048]{1,0:T(8,128)(2,1)} %dy.1, bf16[128,1024]{1,0:T(8,128)(2,1)} %get-tuple-element.26.act, bf16[128,512]{1,0:T(8,128)(2,1)} %get-tuple-element.27.hid), custom_call_target="tpu_custom_call" | custom-call | flops 805306368 | bytes 13631488 | tf_op jit(solution)/shard_map/shared_grads/pallas_call | solution.py:534
  223.3 0.0 copy-done
  223.3 0.8 copy.19
  (2 shorter events, 0.0 us)
Async XLA Ops:
  205.1 18.2 %copy-start = (bf16[2,64,2048]{2,1,0:T(8,128)(2,1)S(1)}, bf16[2,64,2048]{2,1,0:T(8,128)(2,1)}, u32[]{:S(2)}) copy-start(bf16[2,64,2048]{2,1,0:T(8,128)(2,1)} %get-tuple-element.19) | copy-start | bytes 1572868

commit v6 on v5

--- a/solution.py
+++ b/solution.py
@@ -60,9 +60,9 @@
     return found
 
 
-def routed_kernel(x_in, dy_in, table, w_gate, w_up, w_down, s_gate, s_up, s_down,
+def routed_kernel(x_in, dy_in, ids, gates, slots, w_gate, w_up, w_down, s_gate, s_up, s_down,
                   grad_x, x_all, z_all, act_all, hid_all, sact_out, shid_out,
-                  xbuf, dybuf, tbuf, pick, w13, w2, act, hst, xst, zst, sact, shid, sdx,
+                  xbuf, dybuf, tbuf, table, pick, w13, w2, act, hst, xst, zst, sact, shid, sdx,
                   sums, dsend, pbuf, ybuf, cbuf, ebuf,
                   load_sem, out_sem, gs_sem, gr_sem, recv_sem, sy_sem, sd_sem, sown_sem, sz_sem, sx_sem,
                   ds_sem, dr_sem, ys_sem, yr_sem, cs_sem, cr_sem, es_sem, er_sem, credit):
@@ -151,6 +151,14 @@
         def _():
             send_own(q, 0).start()
         send_d(q, z, y, me).start()
+
+    kept = jnp.where(slots[...] >= 0, ids[...], -1)
+    slot_f32 = slots[...].astype(F32) + 1.0
+    for dev in range(16):
+        hits = [kept == 2 * dev + e for e in range(2)]
+        rows = [jnp.sum(jnp.where(hit, gates[...], 0.0), axis=0, keepdims=True) for hit in hits]
+        rows += [jnp.sum(jnp.where(hit, slot_f32, 0.0), axis=0, keepdims=True) - 1.0 for hit in hits]
+        table[dev] = jnp.concatenate(rows + [jnp.zeros((4, tok), F32)], axis=0)
 
     def send_table(d):
         dest = lax.rem(me + d, 16)
@@ -446,7 +454,7 @@
     result.wait()
 
 
-def routed(x_tokens, dy_tokens, table, w_gate, w_up, w_down, s_gate, s_up, s_down):
+def routed(x_tokens, dy_tokens, ids, gates, slots, w_gate, w_up, w_down, s_gate, s_up, s_down):
     tok, dim = x_tokens.shape
     ff = w_gate.shape[2]
     cap = tok // 2
@@ -457,10 +465,10 @@
         name='routed',
         out_shape=(shape((2, cap, dim), BF16), shape((2, 16, cap, dim), BF16), shape((2, 16, cap, dim), BF16),
                    shape((2, 16, cap, 2 * ff), BF16), shape((2, 16, cap, ff), BF16), shape((tok, 2 * ff), BF16), shape((tok, ff), BF16)),
-        in_specs=[ANY, ANY, VMEM] + [ANY] * 6,
+        in_specs=[ANY, ANY] + [VMEM] * 3 + [ANY] * 6,
         out_specs=(ANY,) * 7,
         scratch_shapes=[
-            pltpu.VMEM((16, tok, dim), BF16), pltpu.VMEM((16, tok, dim), BF16), pltpu.VMEM((16, 8, tok), F32), pltpu.VMEM((16, 2 * cap, tok), BF16),
+            pltpu.VMEM((16, tok, dim), BF16), pltpu.VMEM((16, tok, dim), BF16), pltpu.VMEM((16, 8, tok), F32), pltpu.VMEM((16, 8, tok), F32), pltpu.VMEM((16, 2 * cap, tok), BF16),
             pltpu.VMEM((2, dim, 2 * ff), BF16), pltpu.VMEM((2, ff, dim), BF16),
             pltpu.VMEM((2, 16, cap, 2 * ff), BF16), pltpu.VMEM((2, 2, cap, ff), BF16), pltpu.VMEM((2, 2, cap, dim), BF16), pltpu.VMEM((2, 2, cap, dim), BF16),
             pltpu.VMEM((tok, 2 * ff), BF16), pltpu.VMEM((tok, ff), BF16), pltpu.VMEM((tok, dim), F32),
@@ -471,76 +479,81 @@
         ],
         compiler_params=pltpu.CompilerParams(collective_id=0, has_side_effects=True, vmem_limit_bytes=VMEM_LIMIT),
         cost_estimate=pl.CostEstimate(flops=16 * tok * 2 * dim * ff * 5, bytes_accessed=80_000_000, transcendentals=0),
-    )(x_tokens, dy_tokens, table, w_gate, w_up, w_down, s_gate, s_up, s_down)
-
-
-def up_grad_kernel(x, act, g1, g3):
-    ff = g1.shape[2]
-    both = dot_tn(x[0], act[0])
-    g1[0] = both[:, :ff]
-    g3[0] = both[:, ff:]
-
-
-def up_grads(x, act):
-    experts, rows, dim = x.shape
-    ff = act.shape[2] // 2
-    tile = min(512, dim)
-    out = jax.ShapeDtypeStruct((experts, dim, ff), F32)
+    )(x_tokens, dy_tokens, ids, gates, slots, w_gate, w_up, w_down, s_gate, s_up, s_down)
+
+
+def grads_kernel(x_in, dy_in, sact_in, shid_in, xr_in, zr_in, act_in, hid_in,
+                 s1, s3, s2, g1, g3, g2,
+                 x, dy, sact, shid, xr, zr, act, hid, ring, load_sem, ring_sem):
+    dim, ff = x.shape[1], shid.shape[1]
+    tile = ff
+    count = dim // tile
+    small = [pltpu.make_async_copy(a, b, load_sem.at[i]) for i, (a, b) in enumerate(((x_in, x), (sact_in, sact), (shid_in, shid), (dy_in, dy)))]
+    pairs = ((xr_in, xr), (act_in, act), (hid_in, hid), (zr_in, zr))
+
+    def large(e):
+        return [pltpu.make_async_copy(a.at[e], b.at[e], load_sem.at[4 * e + 4 + i]) for i, (a, b) in enumerate(pairs)]
+
+    for cp in small + large(0) + large(1):
+        cp.start()
+    depth = ring.shape[0]
+
+    def drain(slot):
+        for i in range(3):
+            pltpu.make_async_copy(ring.at[slot, i, pl.ds(0, ff), pl.ds(0, ff)], g1.at[0, pl.ds(0, ff), :], ring_sem.at[slot, i]).wait()
+
+    def emit(job, rows, acts, hids, dzs, outs):
+        slot = lax.rem(job, depth)
+
+        @pl.when(job >= depth)
+        def _():
+            drain(slot)
+        both = dot_tn(rows, acts)
+        ring[slot, 0] = both[:, :ff]
+        ring[slot, 1] = both[:, ff:]
+        ring[slot, 2] = dot_tn(hids, dzs)
+        for i in range(3):
+            pltpu.make_async_copy(ring.at[slot, i], outs[i], ring_sem.at[slot, i]).start()
+
+    for cp in small:
+        cp.wait()
+
+    @pl.loop(0, count)
+    def _(i):
+        part = pl.ds(pl.multiple_of(i * tile, tile), tile)
+        emit(i, x[:, part], sact[...], shid[...], dy[:, part], (s1.at[0, part, :], s3.at[0, part, :], s2.at[0, :, part]))
+
+    @pl.loop(0, 2 * count)
+    def _(j):
+        e = lax.div(j, count)
+        i = lax.rem(j, count)
+
+        @pl.when(i == 0)
+        def _():
+            for cp in large(e):
+                cp.wait()
+        part = pl.ds(pl.multiple_of(i * tile, tile), tile)
+        emit(j + count, xr[e, :, part], act[e], hid[e], zr[e, :, part], (g1.at[e, part, :], g3.at[e, part, :], g2.at[e, :, part]))
+    for slot in range(depth):
+        drain(slot)
+
+
+def weight_grads(x, dy, sact, shid, xr, zr, act, hid):
+    dim, ff = x.shape[1], shid.shape[1]
+    tile = ff
+    shape = jax.ShapeDtypeStruct
+    ins = (x, dy, sact, shid, xr, zr, act, hid)
+    dma = pltpu.SemaphoreType.DMA
     return pl.pallas_call(
-        up_grad_kernel,
-        name='up_grads',
-        out_shape=(out, out),
-        grid=(experts, dim // tile),
-        in_specs=[pl.BlockSpec((1, rows, tile), lambda e, i: (e, 0, i)), pl.BlockSpec((1, rows, 2 * ff), lambda e, i: (e, 0, 0))],
-        out_specs=(pl.BlockSpec((1, tile, ff), lambda e, i: (e, i, 0)),) * 2,
+        grads_kernel,
+        name='weight_grads',
+        out_shape=tuple(shape((n,) + d, F32) for n in (1, 2) for d in ((dim, ff), (dim, ff), (ff, dim))),
+        in_specs=[ANY] * 8,
+        out_specs=(ANY,) * 6,
+        scratch_shapes=[pltpu.VMEM(a.shape, a.dtype) for a in ins] + [pltpu.VMEM((4, 3, tile, ff), F32), dma((12,)), dma((4, 3))],
         compiler_params=pltpu.CompilerParams(vmem_limit_bytes=60_000_000),
-        cost_estimate=pl.CostEstimate(flops=4 * experts * rows * dim * ff, bytes_accessed=8 * experts * dim * ff + 2 * x.size + 2 * act.size, transcendentals=0),
-    )(x, act)
-
-
-def down_grad_kernel(hid, dz, g2):
-    g2[0] = dot_tn(hid[0], dz[0])
-
-
-def down_grads(hid, dz):
-    experts, rows, dim = dz.shape
-    ff = hid.shape[2]
-    tile = min(512, dim)
-    return pl.pallas_call(
-        down_grad_kernel,
-        name='down_grads',
-        out_shape=jax.ShapeDtypeStruct((experts, ff, dim), F32),
-        grid=(experts, dim // tile),
-        in_specs=[pl.BlockSpec((1, rows, ff), lambda e, n: (e, 0, 0)), pl.BlockSpec((1, rows, tile), lambda e, n: (e, 0, n))],
-        out_specs=pl.BlockSpec((1, ff, tile), lambda e, n: (e, 0, n)),
-        compiler_params=pltpu.CompilerParams(vmem_limit_bytes=60_000_000),
-        cost_estimate=pl.CostEstimate(flops=2 * experts * rows * dim * ff, bytes_accessed=4 * experts * dim * ff + 2 * hid.size + 2 * dz.size, transcendentals=0),
-    )(hid, dz)
-
-
-def shared_grad_kernel(x, dy, act, hid, g1, g3, g2):
-    ff = hid.shape[1]
-    both = dot_tn(x[...], act[...])
-    g1[0] = both[:, :ff]
-    g3[0] = both[:, ff:]
-    g2[0] = dot_tn(hid[...], dy[...])
-
-
-def shared_grads(x, dy, act, hid):
-    tok, dim = x.shape
-    ff = hid.shape[1]
-    tile = min(512, dim)
-    out = jax.ShapeDtypeStruct((1, dim, ff), F32)
-    return pl.pallas_call(
-        shared_grad_kernel,
-        name='shared_grads',
-        out_shape=(out, out, jax.ShapeDtypeStruct((1, ff, dim), F32)),
-        grid=(dim // tile,),
-        in_specs=[pl.BlockSpec((tok, tile), lambda i: (0, i)), pl.BlockSpec((tok, tile), lambda i: (0, i)), pl.BlockSpec((tok, 2 * ff), lambda i: (0, 0)), pl.BlockSpec((tok, ff), lambda i: (0, 0))],
-        out_specs=(pl.BlockSpec((1, tile, ff), lambda i: (0, i, 0)),) * 2 + (pl.BlockSpec((1, ff, tile), lambda i: (0, 0, i)),),
-        compiler_params=pltpu.CompilerParams(vmem_limit_bytes=60_000_000),
-        cost_estimate=pl.CostEstimate(flops=6 * tok * dim * ff, bytes_accessed=12 * dim * ff + 4 * x.size, transcendentals=0),
-    )(x, dy, act, hid)
+        cost_estimate=pl.CostEstimate(flops=6 * dim * ff * (x.shape[0] + 2 * xr.shape[1]), bytes_accessed=2 * sum(a.size for a in ins) + 36 * dim * ff, transcendentals=0),
+    )(*ins)
 
 
 def solution(mesh):
@@ -553,16 +566,9 @@
     def local_backward(x_tokens, dy_tokens, expert_ids, gate_vals, slot_pos, w_gate, w_up, w_down, shared_gate, shared_up, shared_down):
         tok, dim = x_tokens.shape
         local_experts = w_gate.shape[0]
-        experts = jnp.arange(group * local_experts, dtype=jnp.int32)
-        hit = (expert_ids.T[None] == experts[:, None, None]) & (slot_pos.T[None] >= 0)
-        gates = jnp.sum(jnp.where(hit, gate_vals.T[None], 0.0), axis=1)
-        slots = jnp.sum(jnp.where(hit, slot_pos.T[None].astype(F32) + 1.0, 0.0), axis=1) - 1.0
-        table = jnp.concatenate([gates.reshape(group, local_experts, tok), slots.reshape(group, local_experts, tok), jnp.zeros((group, 8 - 2 * local_experts, tok), F32)], axis=1)
-        grad_x, x_all, z_all, act_all, hid_all, sact, shid = routed(x_tokens, dy_tokens, table, w_gate, w_up, w_down, shared_gate, shared_up, shared_down)
+        grad_x, x_all, z_all, act_all, hid_all, sact, shid = routed(x_tokens, dy_tokens, expert_ids.T, gate_vals.T, slot_pos.T, w_gate, w_up, w_down, shared_gate, shared_up, shared_down)
         x_all, z_all, act_all, hid_all = [a.reshape(local_experts, -1, a.shape[-1]) for a in (x_all, z_all, act_all, hid_all)]
-        grad_w_gate, grad_w_up = up_grads(x_all, act_all)
-        grad_w_down = down_grads(hid_all, z_all)
-        grad_shared_gate, grad_shared_up, grad_shared_down = shared_grads(x_tokens, dy_tokens, sact, shid)
+        grad_shared_gate, grad_shared_up, grad_shared_down, grad_w_gate, grad_w_up, grad_w_down = weight_grads(x_tokens, dy_tokens, sact, shid, x_all, z_all, act_all, hid_all)
         grad_x = grad_x.reshape(tok, dim)
         return grad_x, grad_w_gate, grad_w_up, grad_w_down, grad_shared_gate, grad_shared_up, grad_shared_down
 

time: 225 us -> 216 us (0.960)
  Pallas kernels: 220 us -> 214 us
  other arithmetic: 2.87 us -> 0 us
    pallas_call x3 -> x1, Pallas kernels: 33.9 us -> 28.5 us  [weight_grads(): pl.pallas_call(grads_kernel, name='weight_grads', out_shape=tuple((shape(...]
where the time goes in v6:
time: 216 us
  Pallas kernels  214 us (99%)
    pallas_call x1, Pallas kernels, routed(): pl.pallas_call(routed_kernel, name='routed', out_shape=(shape((2, cap, di...  186 us
    pallas_call x1, Pallas kernels, weight_grads(): pl.pallas_call(grads_kernel, name='weight_grads', out_shape=tuple((shape(...  28.5 us

profile of v6, /device:TPU:0, one launch (start us, length us, event | category | flops | bytes accessed | tf_op | source)
XLA Modules:
  0.0 215.6 jit_solution(2878687434292667720)
XLA Ops:
  0.6 185.6 %routed.1 = (bf16[2,64,2048]{2,1,0:T(8,128)(2,1)}, bf16[2,16,64,2048]{3,2,1,0:T(8,128)(2,1)}, bf16[2,16,64,2048]{3,2,1,0:T(8,128)(2,1)}, bf16[2,16,64,1024]{3,2,...) custom-call(bf16[128,2048]{1,0:T(8,128)(2,1)} %x_in.3, ...), custom_call_target="tpu_custom_call" | custom-call | flops 21474836480 | bytes 80000000 | tf_op jit(solution)/shard_map/routed/pallas_call | solution.py:463
  186.2 0.0 copy-start
  186.2 28.5 %weight_grads.1 = (f32[1,2048,512]{2,1,0:T(8,128)}, f32[1,2048,512]{2,1,0:T(8,128)}, f32[1,512,2048]{2,1,0:T(8,128)}, f32[2,2048,512]{2,1,0:T(8,128)}, f32[2,2048,512]{2,1,0:T(8,128)}, /*index=5*/f32[2,512,2048]{2,1,0:T(8,128)}) custom-call(bf16[128,2048]{1,0:T(8,128)(2,1)} %x_in.3, bf16[128,2048]{1,0:T(8,128)(2,1)} %dy_in.3, ...), custom_call_target="tpu_custom_call" | custom-call | flops 13690208256 | bytes 62259200 | tf_op jit(solution)/shard_map/weight_grads/pallas_call | solution.py:547
  214.8 0.0 copy-done
  214.8 0.8 copy.19
Async XLA Ops:
  186.2 28.5 %copy-start = (bf16[2,64,2048]{2,1,0:T(8,128)(2,1)S(1)}, bf16[2,64,2048]{2,1,0:T(8,128)(2,1)}, u32[]{:S(2)}) copy-start(bf16[2,64,2048]{2,1,0:T(8,128)(2,1)} %get-tuple-element.20) | copy-start | bytes 1572868

commit v7 on v6

--- a/solution.py
+++ b/solution.py
@@ -38,14 +38,14 @@
 
 
 END_PLAN = (
-    'F10F11F20C00F40R00C10F30R10F41X00F21X10C20R20F31C30R30F50X20',
-    'X30C40F51F60R40C50X40Y11F61R50C60R60X50S30F70F71X60C70R70Y21',
-    'X70Y31E00Y20Y10S21S31Y01S20S11S10N00',
+    'C00F20F10F11R00X00F21C10R10C20F40X10F30F31R20F41C30R30C40F60',
+    'X20X30R40F50F51F61X40C50Y01R50C60X50F70F71S30R60C70R70X60Y20',
+    'X70E00Y31Y21Y11Y10S20S31S21S11N00S10',
 )
 MID_PLAN = (
-    'C00F10F30F20R00F31F11C10F50X00F60R10F21C20R20X10F51C30F61F40',
-    'X20F41R30C40R40F70C50X30X40R50F71C60R60Y01X50C70S30Y11X60R70',
-    'X70Y21E00S10Y31N00Y20S21S31Y00S20S11',
+    'C00F20F10R00F30F11C10F31F50X00F21R10C20F60X10F51F40R20C30R30',
+    'F41X20C40R40Y00X30F70C50F61R50X40Y11Y01X50F71C60R60C70R70X60',
+    'X70Y20S30Y31E00S10S20N00Y21S31S21S11',
 )
 
 
@@ -484,18 +484,31 @@
 
 def grads_kernel(x_in, dy_in, sact_in, shid_in, xr_in, zr_in, act_in, hid_in,
                  s1, s3, s2, g1, g3, g2,
-                 x, dy, sact, shid, xr, zr, act, hid, ring, load_sem, ring_sem):
+                 x, dy, sact, shid, xr, zr, act, hid, ring, load_sem, tile_sem, ring_sem):
     dim, ff = x.shape[1], shid.shape[1]
     tile = ff
     count = dim // tile
     small = [pltpu.make_async_copy(a, b, load_sem.at[i]) for i, (a, b) in enumerate(((x_in, x), (sact_in, sact), (shid_in, shid), (dy_in, dy)))]
-    pairs = ((xr_in, xr), (act_in, act), (hid_in, hid), (zr_in, zr))
-
-    def large(e):
-        return [pltpu.make_async_copy(a.at[e], b.at[e], load_sem.at[4 * e + 4 + i]) for i, (a, b) in enumerate(pairs)]
-
-    for cp in small + large(0) + large(1):
+
+    def part(i):
+        return pl.ds(pl.multiple_of(i * tile, tile), tile)
+
+    def whole(e):
+        return [pltpu.make_async_copy(a.at[e], b.at[e], load_sem.at[2 * e + 4 + i]) for i, (a, b) in enumerate(((act_in, act), (hid_in, hid)))]
+
+    def tiles(e, i):
+        return [pltpu.make_async_copy(a.at[e, :, part(i)], b.at[e, :, part(i)], tile_sem.at[n, e, i]) for n, (a, b) in enumerate(((xr_in, xr), (zr_in, zr)))]
+
+    def load(e):
+        for cp in whole(e):
+            cp.start()
+        for i in range(count):
+            for cp in tiles(e, i):
+                cp.start()
+
+    for cp in small:
         cp.start()
+    load(0)
     depth = ring.shape[0]
 
     def drain(slot):
@@ -520,8 +533,8 @@
 
     @pl.loop(0, count)
     def _(i):
-        part = pl.ds(pl.multiple_of(i * tile, tile), tile)
-        emit(i, x[:, part], sact[...], shid[...], dy[:, part], (s1.at[0, part, :], s3.at[0, part, :], s2.at[0, :, part]))
+        emit(i, x[:, part(i)], sact[...], shid[...], dy[:, part(i)], (s1.at[0, part(i), :], s3.at[0, part(i), :], s2.at[0, :, part(i)]))
+    load(1)
 
     @pl.loop(0, 2 * count)
     def _(j):
@@ -530,10 +543,11 @@
 
         @pl.when(i == 0)
         def _():
-            for cp in large(e):
+            for cp in whole(e):
                 cp.wait()
-        part = pl.ds(pl.multiple_of(i * tile, tile), tile)
-        emit(j + count, xr[e, :, part], act[e], hid[e], zr[e, :, part], (g1.at[e, part, :], g3.at[e, part, :], g2.at[e, :, part]))
+        for cp in tiles(e, i):
+            cp.wait()
+        emit(j + count, xr[e, :, part(i)], act[e], hid[e], zr[e, :, part(i)], (g1.at[e, part(i), :], g3.at[e, part(i), :], g2.at[e, :, part(i)]))
     for slot in range(depth):
         drain(slot)
 
@@ -550,7 +564,7 @@
         out_shape=tuple(shape((n,) + d, F32) for n in (1, 2) for d in ((dim, ff), (dim, ff), (ff, dim))),
         in_specs=[ANY] * 8,
         out_specs=(ANY,) * 6,
-        scratch_shapes=[pltpu.VMEM(a.shape, a.dtype) for a in ins] + [pltpu.VMEM((4, 3, tile, ff), F32), dma((12,)), dma((4, 3))],
+        scratch_shapes=[pltpu.VMEM(a.shape, a.dtype) for a in ins] + [pltpu.VMEM((4, 3, tile, ff), F32), dma((8,)), dma((2, 2, dim // tile)), dma((4, 3))],
         compiler_params=pltpu.CompilerParams(vmem_limit_bytes=60_000_000),
         cost_estimate=pl.CostEstimate(flops=6 * dim * ff * (x.shape[0] + 2 * xr.shape[1]), bytes_accessed=2 * sum(a.size for a in ins) + 36 * dim * ff, transcendentals=0),
     )(*ins)

time: 216 us -> 203 us (0.940)
  Pallas kernels: 214 us -> 201 us
    pallas_call x1, Pallas kernels: 186 us -> 174 us  [routed(): pl.pallas_call(routed_kernel, name='routed', out_shape=(shape((2, cap, di...]
where the time goes in v7:
time: 203 us; the launch traced here: 202 us
  Pallas kernels  201 us (99%)
    pallas_call x1, Pallas kernels, routed(): pl.pallas_call(routed_kernel, name='routed', out_shape=(shape((2, cap, di...  174 us
    pallas_call x1, Pallas kernels, weight_grads(): pl.pallas_call(grads_kernel, name='weight_grads', out_shape=tuple((shape(...  26.6 us

profile of v7, /device:TPU:0, one launch (start us, length us, event | category | flops | bytes accessed | tf_op | source)
XLA Modules:
  0.0 202.0 jit_solution(762778407270736930)
XLA Ops:
  0.6 173.9 %routed.1 = (bf16[2,64,2048]{2,1,0:T(8,128)(2,1)}, bf16[2,16,64,2048]{3,2,1,0:T(8,128)(2,1)}, bf16[2,16,64,2048]{3,2,1,0:T(8,128)(2,1)}, bf16[2,16,64,1024]{3,2,...) custom-call(bf16[128,2048]{1,0:T(8,128)(2,1)} %x_in.3, ...), custom_call_target="tpu_custom_call" | custom-call | flops 21474836480 | bytes 80000000 | tf_op jit(solution)/shard_map/routed/pallas_call | solution.py:463
  174.6 0.0 copy-start
  174.6 26.6 %weight_grads.1 = (f32[1,2048,512]{2,1,0:T(8,128)}, f32[1,2048,512]{2,1,0:T(8,128)}, f32[1,512,2048]{2,1,0:T(8,128)}, f32[2,2048,512]{2,1,0:T(8,128)}, f32[2,2048,512]{2,1,0:T(8,128)}, /*index=5*/f32[2,512,2048]{2,1,0:T(8,128)}) custom-call(bf16[128,2048]{1,0:T(8,128)(2,1)} %x_in.3, bf16[128,2048]{1,0:T(8,128)(2,1)} %dy_in.3, ...), custom_call_target="tpu_custom_call" | custom-call | flops 13690208256 | bytes 62259200 | tf_op jit(solution)/shard_map/weight_grads/pallas_call | solution.py:561
  201.2 0.0 copy-done
  201.2 0.8 copy.19
Async XLA Ops:
  174.6 26.6 %copy-start = (bf16[2,64,2048]{2,1,0:T(8,128)(2,1)S(1)}, bf16[2,64,2048]{2,1,0:T(8,128)(2,1)}, u32[]{:S(2)}) copy-start(bf16[2,64,2048]{2,1,0:T(8,128)(2,1)} %get-tuple-element.20) | copy-start | bytes 1572868

commit v8 on v7

--- a/solution.py
+++ b/solution.py
@@ -60,9 +60,9 @@
     return found
 
 
-def routed_kernel(x_in, dy_in, ids, gates, slots, w_gate, w_up, w_down, s_gate, s_up, s_down,
+def routed_kernel(x_in, dy_in, ids_in, gates_in, slots_in, w_gate, w_up, w_down, s_gate, s_up, s_down,
                   grad_x, x_all, z_all, act_all, hid_all, sact_out, shid_out,
-                  xbuf, dybuf, tbuf, table, pick, w13, w2, act, hst, xst, zst, sact, shid, sdx,
+                  xbuf, dybuf, ids, gates, slots, tbuf, table, pick, w13, w2, act, hst, xst, zst, sact, shid, sdx,
                   sums, dsend, pbuf, ybuf, cbuf, ebuf,
                   load_sem, out_sem, gs_sem, gr_sem, recv_sem, sy_sem, sd_sem, sown_sem, sz_sem, sx_sem,
                   ds_sem, dr_sem, ys_sem, yr_sem, cs_sem, cr_sem, es_sem, er_sem, credit):
@@ -114,7 +114,8 @@
     shared_load = weights(1, s_gate, s_up, s_down)
     first_load = weights(0, w_gate.at[0], w_up.at[0], w_down.at[0])
     second_load = weights(1, w_gate.at[1], w_up.at[1], w_down.at[1])
-    for cp in own + shared_load + first_load:
+    routing = [pltpu.make_async_copy(a, b, load_sem.at[8 + i]) for i, (a, b) in enumerate(((ids_in, ids), (gates_in, gates), (slots_in, slots)))]
+    for cp in own + routing + shared_load + first_load:
         cp.start()
 
     barrier = pltpu.get_barrier_semaphore()
@@ -152,6 +153,8 @@
             send_own(q, 0).start()
         send_d(q, z, y, me).start()
 
+    for cp in routing:
+        cp.wait()
     kept = jnp.where(slots[...] >= 0, ids[...], -1)
     slot_f32 = slots[...].astype(F32) + 1.0
     for dev in range(16):
@@ -465,16 +468,17 @@
         name='routed',
         out_shape=(shape((2, cap, dim), BF16), shape((2, 16, cap, dim), BF16), shape((2, 16, cap, dim), BF16),
                    shape((2, 16, cap, 2 * ff), BF16), shape((2, 16, cap, ff), BF16), shape((tok, 2 * ff), BF16), shape((tok, ff), BF16)),
-        in_specs=[ANY, ANY] + [VMEM] * 3 + [ANY] * 6,
+        in_specs=[ANY] * 11,
         out_specs=(ANY,) * 7,
         scratch_shapes=[
-            pltpu.VMEM((16, tok, dim), BF16), pltpu.VMEM((16, tok, dim), BF16), pltpu.VMEM((16, 8, tok), F32), pltpu.VMEM((16, 8, tok), F32), pltpu.VMEM((16, 2 * cap, tok), BF16),
+            pltpu.VMEM((16, tok, dim), BF16), pltpu.VMEM((16, tok, dim), BF16)] + [pltpu.VMEM(a.shape, a.dtype) for a in (ids, gates, slots)] + [
+            pltpu.VMEM((16, 8, tok), F32), pltpu.VMEM((16, 8, tok), F32), pltpu.VMEM((16, 2 * cap, tok), BF16),
             pltpu.VMEM((2, dim, 2 * ff), BF16), pltpu.VMEM((2, ff, dim), BF16),
             pltpu.VMEM((2, 16, cap, 2 * ff), BF16), pltpu.VMEM((2, 2, cap, ff), BF16), pltpu.VMEM((2, 2, cap, dim), BF16), pltpu.VMEM((2, 2, cap, dim), BF16),
             pltpu.VMEM((tok, 2 * ff), BF16), pltpu.VMEM((tok, ff), BF16), pltpu.VMEM((tok, dim), F32),
             pltpu.VMEM((8, tok, dim), F32), pltpu.VMEM((2, tok, dim), F32), pltpu.VMEM((2, tok, dim), F32),
             pltpu.VMEM((4, tok, dim), F32), pltpu.VMEM((2, 3, tok, dim), F32), pltpu.VMEM((2, tok, dim // 2), F32),
-            dma((8,)), dma((4, 8)), dma((16,)), dma((16,)), dma((2, 16)), dma((2, 4)), dma((2, 8)), dma((2, 2)), dma((2, 4)), dma((2,)),
+            dma((11,)), dma((4, 8)), dma((16,)), dma((16,)), dma((2, 16)), dma((2, 4)), dma((2, 8)), dma((2, 2)), dma((2, 4)), dma((2,)),
             dma((2,)), dma((2,)), dma((4, 2)), dma((4, 2)), dma((4, 2)), dma((2, 3, 2)), dma((2,)), dma((2,)), pltpu.SemaphoreType.REGULAR,
         ],
         compiler_params=pltpu.CompilerParams(collective_id=0, has_side_effects=True, vmem_limit_bytes=VMEM_LIMIT),
@@ -499,26 +503,20 @@
     def tiles(e, i):
         return [pltpu.make_async_copy(a.at[e, :, part(i)], b.at[e, :, part(i)], tile_sem.at[n, e, i]) for n, (a, b) in enumerate(((xr_in, xr), (zr_in, zr)))]
 
-    def load(e):
-        for cp in whole(e):
+    first = whole(0) + tiles(0, 0)
+    for cp in first + small:
+        cp.start()
+    for i in range(1, count):
+        for cp in tiles(0, i):
             cp.start()
-        for i in range(count):
-            for cp in tiles(e, i):
-                cp.start()
-
-    for cp in small:
-        cp.start()
-    load(0)
-    depth = ring.shape[0]
+    depth = ring.shape[0] - 2
 
     def drain(slot):
         for i in range(3):
-            pltpu.make_async_copy(ring.at[slot, i, pl.ds(0, ff), pl.ds(0, ff)], g1.at[0, pl.ds(0, ff), :], ring_sem.at[slot, i]).wait()
-
-    def emit(job, rows, acts, hids, dzs, outs):
-        slot = lax.rem(job, depth)
-
-        @pl.when(job >= depth)
+            pltpu.make_async_copy(ring.at[slot, i], g1.at[0, pl.ds(0, ff), :], ring_sem.at[slot, i]).wait()
+
+    def emit(slot, again, rows, acts, hids, dzs, outs):
+        @pl.when(again)
         def _():
             drain(slot)
         both = dot_tn(rows, acts)
@@ -528,14 +526,6 @@
         for i in range(3):
             pltpu.make_async_copy(ring.at[slot, i], outs[i], ring_sem.at[slot, i]).start()
 
-    for cp in small:
-        cp.wait()
-
-    @pl.loop(0, count)
-    def _(i):
-        emit(i, x[:, part(i)], sact[...], shid[...], dy[:, part(i)], (s1.at[0, part(i), :], s3.at[0, part(i), :], s2.at[0, :, part(i)]))
-    load(1)
-
     @pl.loop(0, 2 * count)
     def _(j):
         e = lax.div(j, count)
@@ -547,8 +537,23 @@
                 cp.wait()
         for cp in tiles(e, i):
             cp.wait()
-        emit(j + count, xr[e, :, part(i)], act[e], hid[e], zr[e, :, part(i)], (g1.at[e, part(i), :], g3.at[e, part(i), :], g2.at[e, :, part(i)]))
-    for slot in range(depth):
+        emit(lax.rem(j, depth), j >= depth, xr[e, :, part(i)], act[e], hid[e], zr[e, :, part(i)], (g1.at[e, part(i), :], g3.at[e, part(i), :], g2.at[e, :, part(i)]))
+
+        @pl.when(j == 0)
+        def _():
+            for cp in small:
+                cp.wait()
+            for cp in whole(1):
+                cp.start()
+            for n in range(count):
+                for cp in tiles(1, n):
+                    cp.start()
+
+        @pl.when(lax.rem(j, 2) == 0)
+        def _():
+            k = lax.div(j, 2)
+            emit(depth + lax.rem(k, 2), k >= 2, x[:, part(k)], sact[...], shid[...], dy[:, part(k)], (s1.at[0, part(k), :], s3.at[0, part(k), :], s2.at[0, :, part(k)]))
+    for slot in range(depth + 2):
         drain(slot)
 
 
@@ -557,6 +562,7 @@
     tile = ff
     shape = jax.ShapeDtypeStruct
     ins = (x, dy, sact, shid, xr, zr, act, hid)
+    slots = min(6, 2 + 2 * dim // tile)
     dma = pltpu.SemaphoreType.DMA
     return pl.pallas_call(
         grads_kernel,
@@ -564,7 +570,7 @@
         out_shape=tuple(shape((n,) + d, F32) for n in (1, 2) for d in ((dim, ff), (dim, ff), (ff, dim))),
         in_specs=[ANY] * 8,
         out_specs=(ANY,) * 6,
-        scratch_shapes=[pltpu.VMEM(a.shape, a.dtype) for a in ins] + [pltpu.VMEM((4, 3, tile, ff), F32), dma((8,)), dma((2, 2, dim // tile)), dma((4, 3))],
+        scratch_shapes=[pltpu.VMEM(a.shape, a.dtype) for a in ins] + [pltpu.VMEM((slots, 3, tile, ff), F32), dma((8,)), dma((2, 2, dim // tile)), dma((slots, 3))],
         compiler_params=pltpu.CompilerParams(vmem_limit_bytes=60_000_000),
         cost_estimate=pl.CostEstimate(flops=6 * dim * ff * (x.shape[0] + 2 * xr.shape[1]), bytes_accessed=2 * sum(a.size for a in ins) + 36 * dim * ff, transcendentals=0),
     )(*ins)

time: 203 us -> 203 us (level)
  no operation moved by 1% of the time
where the time goes in v8:
time: 203 us
  Pallas kernels  201 us (99%)
    pallas_call x1, Pallas kernels, routed(): pl.pallas_call(routed_kernel, name='routed', out_shape=(shape((2, cap, di...  173 us
    pallas_call x1, Pallas kernels, weight_grads(): pl.pallas_call(grads_kernel, name='weight_grads', out_shape=tuple((shape(...  27.7 us

profile of v8, /device:TPU:0, one launch (start us, length us, event | category | flops | bytes accessed | tf_op | source)
XLA Modules:
  0.0 202.6 jit_solution(1761819815695974241)
XLA Ops:
  0.6 173.5 %routed.1 = (bf16[2,64,2048]{2,1,0:T(8,128)(2,1)}, bf16[2,16,64,2048]{3,2,1,0:T(8,128)(2,1)}, bf16[2,16,64,2048]{3,2,1,0:T(8,128)(2,1)}, bf16[2,16,64,1024]{3,2,...) custom-call(bf16[128,2048]{1,0:T(8,128)(2,1)} %x_in.3, ...), custom_call_target="tpu_custom_call" | custom-call | flops 21474836480 | bytes 80000000 | tf_op jit(solution)/shard_map/routed/pallas_call | solution.py:466
  174.1 0.0 copy-start
  174.1 27.7 %weight_grads.1 = (f32[1,2048,512]{2,1,0:T(8,128)}, f32[1,2048,512]{2,1,0:T(8,128)}, f32[1,512,2048]{2,1,0:T(8,128)}, f32[2,2048,512]{2,1,0:T(8,128)}, f32[2,2048,512]{2,1,0:T(8,128)}, /*index=5*/f32[2,512,2048]{2,1,0:T(8,128)}) custom-call(bf16[128,2048]{1,0:T(8,128)(2,1)} %x_in.3, bf16[128,2048]{1,0:T(8,128)(2,1)} %dy_in.3, ...), custom_call_target="tpu_custom_call" | custom-call | flops 13690208256 | bytes 62259200 | tf_op jit(solution)/shard_map/weight_grads/pallas_call | solution.py:567
  201.8 0.0 copy-done
  201.9 0.8 copy.19
Async XLA Ops:
  174.1 27.7 %copy-start = (bf16[2,64,2048]{2,1,0:T(8,128)(2,1)S(1)}, bf16[2,64,2048]{2,1,0:T(8,128)(2,1)}, u32[]{:S(2)}) copy-start(bf16[2,64,2048]{2,1,0:T(8,128)(2,1)} %get-tuple-element.20) | copy-start | bytes 1572868

commit v9 on v7

--- a/solution.py
+++ b/solution.py
@@ -60,9 +60,9 @@
     return found
 
 
-def routed_kernel(x_in, dy_in, ids, gates, slots, w_gate, w_up, w_down, s_gate, s_up, s_down,
+def routed_kernel(x_in, dy_in, ids_in, gates_in, slots_in, w_gate, w_up, w_down, s_gate, s_up, s_down,
                   grad_x, x_all, z_all, act_all, hid_all, sact_out, shid_out,
-                  xbuf, dybuf, tbuf, table, pick, w13, w2, act, hst, xst, zst, sact, shid, sdx,
+                  xbuf, dybuf, ids, gates, slots, tbuf, table, pick, w13, w2, act, hst, xst, zst, sact, shid, sdx,
                   sums, dsend, pbuf, ybuf, cbuf, ebuf,
                   load_sem, out_sem, gs_sem, gr_sem, recv_sem, sy_sem, sd_sem, sown_sem, sz_sem, sx_sem,
                   ds_sem, dr_sem, ys_sem, yr_sem, cs_sem, cr_sem, es_sem, er_sem, credit):
@@ -114,7 +114,8 @@
     shared_load = weights(1, s_gate, s_up, s_down)
     first_load = weights(0, w_gate.at[0], w_up.at[0], w_down.at[0])
     second_load = weights(1, w_gate.at[1], w_up.at[1], w_down.at[1])
-    for cp in own + shared_load + first_load:
+    routing = [pltpu.make_async_copy(a, b, load_sem.at[8 + i]) for i, (a, b) in enumerate(((ids_in, ids), (gates_in, gates), (slots_in, slots)))]
+    for cp in own + routing + shared_load + first_load:
         cp.start()
 
     barrier = pltpu.get_barrier_semaphore()
@@ -152,6 +153,8 @@
             send_own(q, 0).start()
         send_d(q, z, y, me).start()
 
+    for cp in routing:
+        cp.wait()
     kept = jnp.where(slots[...] >= 0, ids[...], -1)
     slot_f32 = slots[...].astype(F32) + 1.0
     for dev in range(16):
@@ -465,16 +468,17 @@
         name='routed',
         out_shape=(shape((2, cap, dim), BF16), shape((2, 16, cap, dim), BF16), shape((2, 16, cap, dim), BF16),
                    shape((2, 16, cap, 2 * ff), BF16), shape((2, 16, cap, ff), BF16), shape((tok, 2 * ff), BF16), shape((tok, ff), BF16)),
-        in_specs=[ANY, ANY] + [VMEM] * 3 + [ANY] * 6,
+        in_specs=[ANY] * 11,
         out_specs=(ANY,) * 7,
         scratch_shapes=[
-            pltpu.VMEM((16, tok, dim), BF16), pltpu.VMEM((16, tok, dim), BF16), pltpu.VMEM((16, 8, tok), F32), pltpu.VMEM((16, 8, tok), F32), pltpu.VMEM((16, 2 * cap, tok), BF16),
+            pltpu.VMEM((16, tok, dim), BF16), pltpu.VMEM((16, tok, dim), BF16)] + [pltpu.VMEM(a.shape, a.dtype) for a in (ids, gates, slots)] + [
+            pltpu.VMEM((16, 8, tok), F32), pltpu.VMEM((16, 8, tok), F32), pltpu.VMEM((16, 2 * cap, tok), BF16),
             pltpu.VMEM((2, dim, 2 * ff), BF16), pltpu.VMEM((2, ff, dim), BF16),
             pltpu.VMEM((2, 16, cap, 2 * ff), BF16), pltpu.VMEM((2, 2, cap, ff), BF16), pltpu.VMEM((2, 2, cap, dim), BF16), pltpu.VMEM((2, 2, cap, dim), BF16),
             pltpu.VMEM((tok, 2 * ff), BF16), pltpu.VMEM((tok, ff), BF16), pltpu.VMEM((tok, dim), F32),
             pltpu.VMEM((8, tok, dim), F32), pltpu.VMEM((2, tok, dim), F32), pltpu.VMEM((2, tok, dim), F32),
             pltpu.VMEM((4, tok, dim), F32), pltpu.VMEM((2, 3, tok, dim), F32), pltpu.VMEM((2, tok, dim // 2), F32),
-            dma((8,)), dma((4, 8)), dma((16,)), dma((16,)), dma((2, 16)), dma((2, 4)), dma((2, 8)), dma((2, 2)), dma((2, 4)), dma((2,)),
+            dma((11,)), dma((4, 8)), dma((16,)), dma((16,)), dma((2, 16)), dma((2, 4)), dma((2, 8)), dma((2, 2)), dma((2, 4)), dma((2,)),
             dma((2,)), dma((2,)), dma((4, 2)), dma((4, 2)), dma((4, 2)), dma((2, 3, 2)), dma((2,)), dma((2,)), pltpu.SemaphoreType.REGULAR,
         ],
         compiler_params=pltpu.CompilerParams(collective_id=0, has_side_effects=True, vmem_limit_bytes=VMEM_LIMIT),
@@ -484,7 +488,7 @@
 
 def grads_kernel(x_in, dy_in, sact_in, shid_in, xr_in, zr_in, act_in, hid_in,
                  s1, s3, s2, g1, g3, g2,
-                 x, dy, sact, shid, xr, zr, act, hid, ring, load_sem, tile_sem, ring_sem):
+                 x, dy, sact, shid, xr, zr, act, hid, hid_t, ring, load_sem, tile_sem, ring_sem):
     dim, ff = x.shape[1], shid.shape[1]
     tile = ff
     count = dim // tile
@@ -515,7 +519,7 @@
         for i in range(3):
             pltpu.make_async_copy(ring.at[slot, i, pl.ds(0, ff), pl.ds(0, ff)], g1.at[0, pl.ds(0, ff), :], ring_sem.at[slot, i]).wait()
 
-    def emit(job, rows, acts, hids, dzs, outs):
+    def emit(job, rows, acts, down, outs):
         slot = lax.rem(job, depth)
 
         @pl.when(job >= depth)
@@ -524,7 +528,7 @@
         both = dot_tn(rows, acts)
         ring[slot, 0] = both[:, :ff]
         ring[slot, 1] = both[:, ff:]
-        ring[slot, 2] = dot_tn(hids, dzs)
+        ring[slot, 2] = down()
         for i in range(3):
             pltpu.make_async_copy(ring.at[slot, i], outs[i], ring_sem.at[slot, i]).start()
 
@@ -533,7 +537,7 @@
 
     @pl.loop(0, count)
     def _(i):
-        emit(i, x[:, part(i)], sact[...], shid[...], dy[:, part(i)], (s1.at[0, part(i), :], s3.at[0, part(i), :], s2.at[0, :, part(i)]))
+        emit(i, x[:, part(i)], sact[...], lambda: dot_tn(shid[...], dy[:, part(i)]), (s1.at[0, part(i), :], s3.at[0, part(i), :], s2.at[0, :, part(i)]))
     load(1)
 
     @pl.loop(0, 2 * count)
@@ -545,9 +549,10 @@
         def _():
             for cp in whole(e):
                 cp.wait()
+            hid_t[...] = hid[e].T
         for cp in tiles(e, i):
             cp.wait()
-        emit(j + count, xr[e, :, part(i)], act[e], hid[e], zr[e, :, part(i)], (g1.at[e, part(i), :], g3.at[e, part(i), :], g2.at[e, :, part(i)]))
+        emit(j + count, xr[e, :, part(i)], act[e], lambda: dot_nn(hid_t[...], zr[e, :, part(i)]), (g1.at[e, part(i), :], g3.at[e, part(i), :], g2.at[e, :, part(i)]))
     for slot in range(depth):
         drain(slot)
 
@@ -564,7 +569,7 @@
         out_shape=tuple(shape((n,) + d, F32) for n in (1, 2) for d in ((dim, ff), (dim, ff), (ff, dim))),
         in_specs=[ANY] * 8,
         out_specs=(ANY,) * 6,
-        scratch_shapes=[pltpu.VMEM(a.shape, a.dtype) for a in ins] + [pltpu.VMEM((4, 3, tile, ff), F32), dma((8,)), dma((2, 2, dim // tile)), dma((4, 3))],
+        scratch_shapes=[pltpu.VMEM(a.shape, a.dtype) for a in ins] + [pltpu.VMEM((ff, hid.shape[1]), BF16), pltpu.VMEM((4, 3, tile, ff), F32), dma((8,)), dma((2, 2, dim // tile)), dma((4, 3))],
         compiler_params=pltpu.CompilerParams(vmem_limit_bytes=60_000_000),
         cost_estimate=pl.CostEstimate(flops=6 * dim * ff * (x.shape[0] + 2 * xr.shape[1]), bytes_accessed=2 * sum(a.size for a in ins) + 36 * dim * ff, transcendentals=0),
     )(*ins)

time: 203 us -> 203 us (level)
  no operation moved by 1% of the time
where the time goes in v9:
time: 203 us; the launch traced here: 202 us
  Pallas kernels  201 us (99%)
    pallas_call x1, Pallas kernels, routed(): pl.pallas_call(routed_kernel, name='routed', out_shape=(shape((2, cap, di...  173 us
    pallas_call x1, Pallas kernels, weight_grads(): pl.pallas_call(grads_kernel, name='weight_grads', out_shape=tuple((shape(...  27.1 us

profile of v9, /device:TPU:0, one launch (start us, length us, event | category | flops | bytes accessed | tf_op | source)
XLA Modules:
  0.0 202.0 jit_solution(3309683955399985157)
XLA Ops:
  0.6 173.5 %routed.1 = (bf16[2,64,2048]{2,1,0:T(8,128)(2,1)}, bf16[2,16,64,2048]{3,2,1,0:T(8,128)(2,1)}, bf16[2,16,64,2048]{3,2,1,0:T(8,128)(2,1)}, bf16[2,16,64,1024]{3,2,...) custom-call(bf16[128,2048]{1,0:T(8,128)(2,1)} %x_in.3, ...), custom_call_target="tpu_custom_call" | custom-call | flops 21474836480 | bytes 80000000 | tf_op jit(solution)/shard_map/routed/pallas_call | solution.py:466
  174.1 0.0 copy-start
  174.1 27.1 %weight_grads.1 = (f32[1,2048,512]{2,1,0:T(8,128)}, f32[1,2048,512]{2,1,0:T(8,128)}, f32[1,512,2048]{2,1,0:T(8,128)}, f32[2,2048,512]{2,1,0:T(8,128)}, f32[2,2048,512]{2,1,0:T(8,128)}, /*index=5*/f32[2,512,2048]{2,1,0:T(8,128)}) custom-call(bf16[128,2048]{1,0:T(8,128)(2,1)} %x_in.3, bf16[128,2048]{1,0:T(8,128)(2,1)} %dy_in.3, ...), custom_call_target="tpu_custom_call" | custom-call | flops 13690208256 | bytes 62259200 | tf_op jit(solution)/shard_map/weight_grads/pallas_call | solution.py:566
  201.2 0.0 copy-done
  201.2 0.8 copy.19
Async XLA Ops:
  174.1 27.1 %copy-start = (bf16[2,64,2048]{2,1,0:T(8,128)(2,1)S(1)}, bf16[2,64,2048]{2,1,0:T(8,128)(2,1)}, u32[]{:S(2)}) copy-start(bf16[2,64,2048]{2,1,0:T(8,128)(2,1)} %get-tuple-element.20) | copy-start | bytes 1572868
